TPU v7x, 32 devices: a whole 2x2x4 slice. The times are simulated.
32 devices in a mesh: gx: 4 (over y, core), gy: 8 (over z, x).
Axes of the slice: x: 2, y: 2, z: 4, core: 2. Of those that a mesh axis runs over, the one named last changes fastest.
Arguments:
- source: float32 [64, 16, 1024], P(None, 'gx', 'gy'), may hold values from -6 to 6
- initial: float32 [64, 16, 1024], P(None, 'gx', 'gy'), may hold values from -6 to 6
- reaction: float32 [64, 16, 1024], P(None, 'gx', 'gy'), may hold values from 1 to 3
- stiffness: float32 [16, 1024], P('gx', 'gy'), may hold values from 0.5 to 2
- line_op: float32 [8, 8], replicated, may hold values from -1.6 to 5.6
- face_deriv: float32 [8], replicated, may hold values from -2 to 2
- wall_flags: int32 [4, 16, 1024], P(None, 'gx', 'gy'), may hold values 0 or 1
Outputs:
- hessenberg: float32 [6, 5], replicated
- krylov_basis: float32 [6, 64, 16, 1024], P(None, None, 'gx', 'gy')
All inputs are finite; a program needn't handle non-finite values. No bound on the sum of `wall_flags` on one device may be relied on, other than what follows from the above.
Results may differ from a plain program's by a relative error of at most 0.0003.
Values sent between devices are 32-bit elements; how exact they have to be, the bound alone decides.
A program may use at most 64 MiB of HBM per device.

v0:
```python
import functools

import jax
import jax.numpy as jnp
from jax import lax
from jax.experimental import pallas as pl
from jax.experimental.pallas import tpu as pltpu
from jax.sharding import PartitionSpec as P

P_SIZE = 8
ITERS = 5
VECS = ITERS + 1
TAU = 2.0
FLOOR = 0.1
PAIRS = P_SIZE // 2
SLOT = 32
GHOST = 8
WIDE = 3 * P_SIZE + 4
NARROW = 3 * 2 + 1
MESH = pl.DeviceIdType.MESH


def block_offsets(nx):
    near = min(nx, 5)
    return list(range(-((near - 1) // 2), near // 2 + 1))


def kernel(
    nx, ny, total,
    line, deriv, src_any, ini_any, rea_any, stf, wal,
    hess_out, bas,
    coef, gcoef, scoef, sgcoef, small, src, ini, rea,
    wide, low_send, high_send, south_in, north_in,
    page_ini, page_src, page_rea, page_small, page_a, page_b, patch,
    in_sem, hsend, hrecv, rsend, rrecv,
    hs_sem, hr_sem, ws_sem, wr_sem, ns_sem, nr_sem, rs_sem, rr_sem,
):
    n = nx * ny
    offs = block_offsets(nx)
    blocks = len(offs)
    here = offs.index(0)
    gx, gy = lax.axis_index("gx"), lax.axis_index("gy")
    me = gx * ny + gy

    side = gy // (ny // 2)
    offsets = sorted(range(1, nx), key=lambda d: abs(2 * d - nx))

    def for_peers(act):
        def column(k, own_column):
            across = side * k + (1 - side) * (ny - 1 - k)
            for d in offsets:
                act((lax.rem(gx + d, nx), across))
            if own_column:
                skip = jnp.where(k >= (side * gy + (1 - side) * (ny - 1 - gy)), 1, 0)
                act((gx, across + (2 * side - 1) * skip))

        if n <= 64:
            for k in range(ny - 1):
                column(k, True)
        else:
            lax.fori_loop(0, ny - 1, lambda k, c: (column(k, True), c)[1], 0)
        column(ny - 1, False)

    def at(dx, dy):
        return (lax.rem(gx + dx + nx, nx), lax.rem(gy + dy + ny, ny))

    barrier = pltpu.get_barrier_semaphore()

    def greet(device):
        pl.semaphore_signal(barrier, inc=1, device_id=device, device_id_type=MESH)

    loads = [
        pltpu.make_async_copy(given, held, in_sem.at[k])
        for k, (given, held) in enumerate(((ini_any, ini), (src_any, src), (rea_any, rea)))
    ]
    for load in loads:
        load.start()
    for_peers(greet)

    sub = lax.broadcasted_iota(jnp.int32, (8, 128), 0)
    lane = lax.broadcasted_iota(jnp.int32, (8, 128), 1)
    low = sub < 4
    xpos = sub % 4
    slot_of = lane // SLOT
    in_slot = lane % SLOT
    south_half = in_slot < SLOT // 2
    group_of = in_slot // GHOST

    def srl(v, s):
        s = s % 8
        return v if s == 0 else pltpu.roll(v, s, 0)

    def lrl(v, s):
        s = s % 128
        return v if s == 0 else pltpu.roll(v, s, 1)

    def halves(a, b):
        return jnp.where(low, a, b)

    def by_slot(parts):
        out = parts[0]
        for p in range(1, PAIRS):
            out = jnp.where(slot_of == p, parts[p], out)
        return out

    def dot(pairs):
        out = None
        for c, v in pairs:
            out = c * v if out is None else out + c * v
        return out

    mix = {}
    for p in range(PAIRS):
        for r in range(PAIRS):
            mix[p, r, 0] = halves(line[2 * p, 2 * r], line[2 * p + 1, 2 * r + 1])
            mix[p, r, 1] = halves(line[2 * p, 2 * r + 1], line[2 * p + 1, 2 * r])
            for k in range(2):
                coef[(p * PAIRS + r) * 2 + k] = mix[p, r, k]
    glow = [0.5 * deriv[c] + (TAU if c == 0 else 0.0) for c in range(P_SIZE)]
    gupp = [
        0.5 * deriv[P_SIZE - 1 - c] + (TAU if c == P_SIZE - 1 else 0.0) for c in range(P_SIZE)
    ]
    lows = [halves(glow[2 * p], glow[2 * p + 1]) for p in range(PAIRS)]
    upps = [halves(gupp[2 * p], gupp[2 * p + 1]) for p in range(PAIRS)]
    for p in range(PAIRS):
        gcoef[p] = lows[p]
        gcoef[PAIRS + p] = upps[p]
    small[0, 0:4] = stf[...]
    small[0, 4:8] = stf[...]
    opened = [1.0 - wal[f].astype(jnp.float32) for f in range(4)]
    for slot, (first, second) in enumerate(((0, 0), (1, 1), (2, 3))):
        small[slot + 1, 0:4] = opened[first]
        small[slot + 1, 4:8] = opened[second]
    trace = line[0, 0]
    for c in range(1, P_SIZE):
        trace = trace + line[c, c]
    shift = 3.0 + 0.25 * trace

    def tile(ref, a, p):
        return ref[pl.ds((a * PAIRS + p) * 8, 8), :]

    def put(ref, a, p, value):
        ref[pl.ds((a * PAIRS + p) * 8, 8), :] = value

    def tiles():
        return [(a, p) for a in range(P_SIZE) for p in range(PAIRS)]

    def xfaces(get):
        fw, fe = [], []
        for p in range(PAIRS):
            vs = [get(c, p) for c in range(P_SIZE)]
            fw.append(dot(zip(glow, vs)))
            fe.append(dot(zip(gupp, vs)))
        return fw, fe

    def halo_copy(slot, way, device):
        return pltpu.make_async_remote_copy(
            src_ref=hsend.at[slot, way],
            dst_ref=hrecv.at[slot, way],
            send_sem=hs_sem.at[slot, way],
            recv_sem=hr_sem.at[slot, way],
            device_id=device,
            device_id_type=MESH,
        )

    def send_halo(slot, faces, ready=lambda: None):
        fw, fe = faces
        cw, ce = fw[0], srl(fe[0], -3)
        for p in range(1, PAIRS):
            cw = jnp.where(xpos == p, srl(fw[p], p), cw)
            ce = jnp.where(xpos == p, srl(fe[p], p - 3), ce)
        hsend[slot, 0] = cw
        hsend[slot, 1] = ce
        ready()
        copies = [halo_copy(slot, 0, at(-1, 0)), halo_copy(slot, 1, at(1, 0))]
        for copy in copies:
            copy.start()
        return copies

    def take_halo(slot, copies, sign):
        for copy in copies:
            copy.wait_recv()
        cw, ce = hrecv[slot, 0], hrecv[slot, 1]
        open_w, open_e = small[1] * sign, small[2] * sign
        first = [open_w * jnp.where(xpos == 0, srl(ce, -p), 0.0) for p in range(PAIRS)]
        last = [open_e * jnp.where(xpos == 3, srl(cw, 3 - p), 0.0) for p in range(PAIRS)]
        return first, last

    def operate(get, faces, moved, emit):
        fw, fe = faces
        stiff, open_w, open_e, open_y = small[0], small[1], small[2], small[3]
        sides = {}
        for p in range(PAIRS):
            nb_e = jnp.where(xpos == 3, 0.0, srl(fw[p], 7))
            nb_w = jnp.where(xpos == 0, 0.0, srl(fe[p], 1))
            sides[0, p] = fw[p] - open_w * nb_w
            sides[P_SIZE - 1, p] = fe[p] - open_e * nb_e
        for a in range(P_SIZE):
            vs = [get(a, p) for p in range(PAIRS)]
            ss = [srl(v, 4) for v in vs]
            s = dot((gcoef[p], vs[p]) for p in range(PAIRS))
            t = dot((gcoef[PAIRS + p], vs[p]) for p in range(PAIRS))
            own = halves(s, t) + srl(halves(t, s), 4)
            q = srl(own, 4)
            term = own - open_y * halves(lrl(q, 1), lrl(q, 127))
            for p in range(PAIRS):
                acc = None
                for r in range(PAIRS):
                    k = (p * PAIRS + r) * 2
                    part = coef[k] * vs[r] + coef[k + 1] * ss[r]
                    acc = part if acc is None else acc + part
                other = dot((line[a, c], get(c, p)) for c in range(P_SIZE))
                react = tile(rea, a, p) - shift if moved else tile(rea, a, p)
                value = react * vs[p] + stiff * (acc + other)
                if p == 0:
                    value = value + jnp.where(low, term, 0.0)
                if p == PAIRS - 1:
                    value = value + jnp.where(low, 0.0, term)
                if (a, p) in sides:
                    value = value + sides[a, p]
                emit(a, p, value)

    def gather_rows(accs):
        zero = jnp.zeros((8, 128), jnp.float32)
        level = list(accs) + [zero] * (8 - len(accs))
        for step in (1, 2, 4):
            keep = (sub // step) % 2 == 0
            level = [
                jnp.where(keep, level[i], level[i + 1])
                + srl(jnp.where(keep, level[i + 1], level[i]), step)
                for i in range(0, len(level), 2)
            ]
        return level[0]

    def fold(v):
        for step in (4, 2, 1):
            v = v + srl(v, step)
        return v

    def row_copy(slot, device):
        return pltpu.make_async_remote_copy(
            src_ref=rsend.at[slot],
            dst_ref=rrecv.at[slot, pl.ds(me, 1)],
            send_sem=rs_sem.at[slot],
            recv_sem=rr_sem.at[slot],
            device_id=device,
            device_id_type=MESH,
        )

    def pack_sums(accs, start):
        sums = jnp.sum(gather_rows(accs), axis=1, keepdims=True)
        return jnp.where(lane == sub + start, sums, 0.0)

    def start_reduce(slot, packed):
        row = fold(packed)[0:1]
        rsend[slot] = row
        rrecv[slot, pl.ds(me, 1)] = row
        for_peers(lambda device: row_copy(slot, device).start())

    def end_reduce(slot):
        block = rrecv.at[slot, pl.ds(0, n - 1)]
        pltpu.make_async_copy(block, block, rr_sem.at[slot]).wait()
        value = rrecv[slot, 0:8]
        for g in range(1, n // 8):
            value = value + rrecv[slot, 8 * g:8 * g + 8]
        value = fold(value)
        return lambda k: jnp.broadcast_to(value[:, k:k + 1], (8, 128))

    fields = ((ini, 0), (src, 1), (rea, 2))

    def narrow_copy(sent, held, back, dx, dy):
        j = offs.index(back)
        return pltpu.make_async_remote_copy(
            src_ref=sent,
            dst_ref=held.at[j],
            send_sem=ns_sem.at[0 if dy < 0 else 1, j],
            recv_sem=nr_sem.at[0 if dy < 0 else 1, j],
            device_id=at(dx, dy),
            device_id_type=MESH,
        )

    def opposite(o):
        return -o if -o in offs else o

    def wide_copy(o):
        j = offs.index(opposite(o))
        return pltpu.make_async_remote_copy(
            src_ref=wide.at[here],
            dst_ref=wide.at[j],
            send_sem=ws_sem.at[j],
            recv_sem=wr_sem.at[j],
            device_id=at(o, 0),
            device_id_type=MESH,
        )

    def pack_edges():
        def gathered(parts):
            return by_slot([lrl(parts[p], 16 + SLOT * p) for p in range(PAIRS)])

        def narrow(items, index):
            for ref, start in ((low_send, 16), (high_send, 8)):
                out = None
                for i, v in enumerate(items):
                    moved = lrl(v, GHOST * i - start)
                    out = moved if out is None else jnp.where(group_of == i, moved, out)
                ref[index] = out

        for ref, f in fields:
            for quad in range(2):
                items = []
                for a in range(4 * quad, 4 * quad + 4):
                    v = gathered([tile(ref, a, p) for p in range(PAIRS)])
                    wide[here, f * P_SIZE + a] = v
                    items.append(v)
                narrow(items, f * 2 + quad)
        items = []
        for f in range(4):
            v = gathered([small[f]] * PAIRS)
            wide[here, 3 * P_SIZE + f] = v
            items.append(v)
        narrow(items, 6)

    narrow_copies = [
        narrow_copy(low_send, north_in, opposite(o), o, -1) for o in offs
    ] + [
        narrow_copy(high_send, south_in, opposite(o), o, 1) for o in offs
    ]
    wide_copies = [wide_copy(o) for o in sorted(offs, key=abs) if o]

    for d in range(PAIRS):
        for k in range(2):
            scoef[2 * d + k] = by_slot([mix[(r + d) % PAIRS, r, k] for r in range(PAIRS)])
    sgcoef[0] = by_slot(lows)
    sgcoef[1] = by_slot(upps)
    y_mask = (low & (slot_of == 0)) | (~low & (slot_of == PAIRS - 1))

    def unpack_pages():
        def merge(seam, wide_part, narrow_part, i):
            if seam == 0:
                return jnp.where(south_half, lrl(narrow_part, GHOST - GHOST * i), wide_part)
            return jnp.where(south_half, wide_part, lrl(narrow_part, 16 - GHOST * i))

        for seam, narrow_in in ((0, south_in), (1, north_in)):
            for j in range(blocks):
                for f, page in enumerate((page_ini, page_src, page_rea)):
                    for a in range(P_SIZE):
                        page[seam, j * P_SIZE + a] = merge(
                            seam, wide[j, f * P_SIZE + a], narrow_in[j, f * 2 + a // 4], a % 4
                        )
                for f in range(4):
                    page_small[seam, j * 4 + f] = merge(
                        seam, wide[j, 3 * P_SIZE + f], narrow_in[j, 6], f
                    )

    def page_level(level):
        given = page_ini if level == 0 else (page_a if level % 2 else page_b)
        out = page_b if level % 2 else page_a

        def seam_body(seam, carry):
            fw, fe = [], []
            for j in range(blocks):
                vs = [given[seam, j * P_SIZE + a] for a in range(P_SIZE)]
                fw.append(dot(zip(glow, vs)))
                fe.append(dot(zip(gupp, vs)))
            for j in range(blocks):
                stiff, open_w, open_e, open_y = [page_small[seam, j * 4 + f] for f in range(4)]
                nb_e = jnp.where(xpos == 3, srl(fw[(j + 1) % blocks], 3), srl(fw[j], 7))
                nb_w = jnp.where(xpos == 0, srl(fe[(j - 1) % blocks], 5), srl(fe[j], 1))
                sides = {
                    0: fw[j] - open_w * nb_w,
                    P_SIZE - 1: fe[j] - open_e * nb_e,
                }
                vs = [given[seam, j * P_SIZE + a] for a in range(P_SIZE)]
                for a in range(P_SIZE):
                    v = vs[a]
                    ss = srl(v, 4)
                    acc = scoef[0] * v + scoef[1] * ss
                    for d in range(1, PAIRS):
                        acc = acc + lrl(scoef[2 * d] * v + scoef[2 * d + 1] * ss, SLOT * d)
                    s, t = sgcoef[0] * v, sgcoef[1] * v
                    own = halves(s, t) + srl(halves(t, s), 4)
                    own = own + lrl(own, 64)
                    own = own + lrl(own, 32)
                    q = srl(own, 4)
                    term = own - open_y * halves(lrl(q, 1), lrl(q, 127))
                    other = dot(zip([line[a, c] for c in range(P_SIZE)], vs))
                    react = page_rea[seam, j * P_SIZE + a]
                    if level:
                        react = react - shift
                    value = react * v + stiff * (acc + other) + jnp.where(y_mask, term, 0.0)
                    if a in sides:
                        value = value + sides[a]
                    if level == 0:
                        value = page_src[seam, j * P_SIZE + a] - value
                    out[seam, j * P_SIZE + a] = value
            return carry

        lax.fori_loop(0, 2, seam_body, 0)
        for a in range(P_SIZE):
            k = here * P_SIZE + a
            patch[level, a] = jnp.where(south_half, out[1, k], out[0, k])

    edge = (lane < VECS) | (lane >= 128 - VECS)

    def patched(level, a, p, v):
        return jnp.where(edge, lrl(patch[level, a], 112 - SLOT * p), v)

    started = []

    loads[0].wait()
    get = functools.partial(tile, ini)
    faces = xfaces(get)
    copies = send_halo(0, faces, lambda: pl.semaphore_wait(barrier, n - 1))
    started += copies
    loads[1].wait()
    loads[2].wait()
    y0 = bas.at[0]
    operate(get, faces, False, lambda a, p, v: put(y0, a, p, tile(src, a, p) - v))
    pack_edges()
    for copy in narrow_copies:
        copy.start()

    ways = len(wide_copies)
    for level in range(ITERS):
        now = bas.at[level]
        get = functools.partial(tile, now)
        fw, fe = xfaces(get)
        first, last = take_halo(level, copies, 1.0 if level == 0 else -1.0)
        fw = [fw[p] + glow[0] * first[p] + glow[P_SIZE - 1] * last[p] for p in range(PAIRS)]
        fe = [fe[p] + gupp[0] * first[p] + gupp[P_SIZE - 1] * last[p] for p in range(PAIRS)]
        copies = send_halo(level + 1, (fw, fe))
        started += copies
        for p in range(PAIRS):
            put(now, 0, p, get(0, p) + first[p])
            put(now, P_SIZE - 1, p, get(P_SIZE - 1, p) + last[p])
        operate(get, (fw, fe), True, functools.partial(put, bas.at[level + 1]))
        if level == 0:
            for copy in wide_copies[:ways - ways // 2]:
                copy.start()
        if level == 1:
            for copy in wide_copies[ways - ways // 2:]:
                copy.start()
            accs = [None] * 3
            for a, p in tiles():
                u, v = tile(bas.at[0], a, p), tile(bas.at[1], a, p)
                new = [u * u, u * v, v * v]
                accs = new if accs[0] is None else [s + t for s, t in zip(accs, new)]
            start_reduce(0, pack_sums(accs, 0))
        if level == 3:
            for copy in narrow_copies + wide_copies:
                copy.wait_recv()
            unpack_pages()
            for k in range(3):
                page_level(k)
        if level == 4:
            for k in range(3, VECS):
                page_level(k)

    sums = end_reduce(0)
    size = jnp.maximum(sums(0), 1e-30)
    mean = sums(1) / size
    spread = jnp.sqrt(jnp.maximum(sums(2) / size - mean * mean, 0.0)) + 0.1
    inv = 1.0 / spread
    ratio = mean * inv
    theta = shift + mean
    powers = [None, inv]
    for k in range(2, VECS):
        powers.append(powers[k - 1] * inv)

    pairs = [(i, j) for j in range(ITERS) for i in range(j + 1)]
    accs, tail = None, None
    for a, p in tiles():
        lev = []
        for k in range(VECS):
            v = patched(k, a, p, tile(bas.at[k], a, p))
            lev.append(v if k == 0 else v * powers[k])
        vecs = [lev[0]]
        for k in range(1, VECS):
            lev = [lev[i + 1] - ratio * lev[i] for i in range(len(lev) - 1)]
            vecs.append(lev[0])
        for k in range(1, VECS):
            put(bas.at[k], a, p, vecs[k])
        put(bas.at[0], a, p, vecs[0])
        new = [vecs[i] * vecs[j] for i, j in pairs]
        accs = new if accs is None else [s + t for s, t in zip(accs, new)]
        if 0 < a < P_SIZE - 1:
            new = [v * vecs[ITERS] for v in vecs]
            tail = new if tail is None else [s + t for s, t in zip(tail, new)]
    packed = pack_sums(accs[:8], 0) + pack_sums(accs[8:], 8)

    first, last = take_halo(ITERS, copies, -1.0)
    for a, extra in ((0, first), (P_SIZE - 1, last)):
        for p in range(PAIRS):
            v = tile(bas.at[ITERS], a, p) + jnp.where(edge, 0.0, extra[p] * powers[ITERS])
            put(bas.at[ITERS], a, p, v)
            vecs = [tile(bas.at[k], a, p) for k in range(ITERS)] + [v]
            tail = [s + u * v for s, u in zip(tail, vecs)]
    start_reduce(1, packed + pack_sums(tail, 16))
    sums = end_reduce(1)

    gram = {}
    for k, (i, j) in enumerate(pairs):
        gram[i, j] = sums(k) * (1.0 / total)
    for i in range(VECS):
        gram[i, ITERS] = sums(16 + i) * (1.0 / total)

    def times_gram(u, rows):
        return [
            dot((gram[min(i, r), max(i, r)], u[i]) for i in range(len(u))) for r in range(rows)
        ]

    hess = jnp.zeros((8, 128), jnp.float32)
    combos = [[1.0 / jnp.sqrt(gram[0, 0] + FLOOR)]]
    for j in range(ITERS):
        c = combos[j]
        u = [theta * c[0]]
        for i in range(1, j + 1):
            u.append(spread * c[i - 1] + theta * c[i])
        u.append(spread * c[j])
        g = times_gram(u, j + 1)
        rest = list(u)
        for i in range(j + 1):
            h = dot(zip(combos[i], g))
            hess = jnp.where((sub == i) & (lane == j), h, hess)
            for k in range(i + 1):
                rest[k] = rest[k] - h * combos[i][k]
        square = dot(zip(rest, times_gram(rest, j + 2)))
        beta = jnp.sqrt(jnp.maximum(square, 0.0) + FLOOR)
        hess = jnp.where((sub == j + 1) & (lane == j), beta, hess)
        post = 1.0 / beta
        combos.append([r * post for r in rest])

    for a, p in tiles():
        vecs = [tile(bas.at[k], a, p) for k in range(VECS)]
        for j in reversed(range(VECS)):
            put(bas.at[j], a, p, dot(zip(combos[j], vecs)))
    hess_out[...] = hess[0:VECS, 0:ITERS]

    for copy in started + narrow_copies + wide_copies:
        copy.wait_send()
    for slot in range(2):
        block = rrecv.at[slot, pl.ds(0, n - 1)]
        pltpu.make_async_copy(block, block, rs_sem.at[slot]).wait()


def store(hess, basis, hess_out, basis_out, sem):
    copies = [
        pltpu.make_async_copy(basis, basis_out, sem.at[0]),
        pltpu.make_async_copy(hess, hess_out, sem.at[1]),
    ]
    for copy in copies:
        copy.start()
    for copy in copies:
        copy.wait()


def body(nx, ny, source, initial, reaction, stiffness, line_op, face_deriv, wall_flags):
    nodes, ex, ey = source.shape
    n = nx * ny
    rows = nodes * ex
    flat = (rows, ey)
    blocks = len(block_offsets(nx))
    total = float(nodes * ex * nx * ey * ny)
    vmem = pl.BlockSpec(memory_space=pltpu.VMEM)
    hbm = pl.BlockSpec(memory_space=pl.ANY)
    smem = pl.BlockSpec(memory_space=pltpu.SMEM)

    def array(*lead):
        return pltpu.VMEM(lead + (8, 128), jnp.float32)

    dma = pltpu.SemaphoreType.DMA
    hess, basis = pl.pallas_call(
        functools.partial(kernel, nx, ny, total),
        out_shape=(
            pltpu.VMEM((VECS, ITERS), jnp.float32),
            pltpu.VMEM((VECS,) + flat, jnp.float32),
        ),
        in_specs=[smem, smem, hbm, hbm, hbm, vmem, vmem],
        out_specs=(vmem, vmem),
        scratch_shapes=[
            array(2 * PAIRS * PAIRS),
            array(2 * PAIRS),
            array(2 * PAIRS),
            array(2),
            array(4),
            pltpu.VMEM(flat, jnp.float32),
            pltpu.VMEM(flat, jnp.float32),
            pltpu.VMEM(flat, jnp.float32),
            array(blocks, WIDE),
            array(NARROW),
            array(NARROW),
            array(blocks, NARROW),
            array(blocks, NARROW),
            array(2, blocks * P_SIZE),
            array(2, blocks * P_SIZE),
            array(2, blocks * P_SIZE),
            array(2, blocks * 4),
            array(2, blocks * P_SIZE),
            array(2, blocks * P_SIZE),
            array(VECS, P_SIZE),
            dma((3,)),
            array(VECS, 2),
            array(VECS, 2),
            pltpu.VMEM((2, 1, 128), jnp.float32),
            pltpu.VMEM((2, n, 128), jnp.float32),
            dma((VECS, 2)),
            dma((VECS, 2)),
            dma((blocks,)),
            dma((blocks,)),
            dma((2, blocks)),
            dma((2, blocks)),
            dma((2,)),
            dma((2,)),
        ],
        compiler_params=pltpu.CompilerParams(collective_id=0, has_side_effects=True),
    )(
        line_op, face_deriv, source.reshape(flat), initial.reshape(flat), reaction.reshape(flat),
        stiffness, wall_flags,
    )
    hess = pltpu.with_memory_space_constraint(hess, pltpu.VMEM)
    basis = pltpu.with_memory_space_constraint(basis, pltpu.VMEM)
    hess, basis = pl.pallas_call(
        store,
        out_shape=(
            jax.ShapeDtypeStruct(hess.shape, jnp.float32),
            jax.ShapeDtypeStruct(basis.shape, jnp.float32),
        ),
        in_specs=[hbm, hbm],
        out_specs=(hbm, hbm),
        scratch_shapes=[pltpu.SemaphoreType.DMA((2,))],
    )(hess, basis)
    return hess, basis.reshape((VECS, nodes, ex, ey))


def solution(mesh):
    return jax.shard_map(
        functools.partial(body, mesh.shape["gx"], mesh.shape["gy"]),
        mesh=mesh,
        in_specs=(
            P(None, "gx", "gy"),
            P(None, "gx", "gy"),
            P(None, "gx", "gy"),
            P("gx", "gy"),
            P(),
            P(),
            P(None, "gx", "gy"),
        ),
        out_specs=(P(), P(None, None, "gx", "gy")),
        check_vma=False,
    )
```

profile of v0, /device:TPU:0, one launch (start us, length us, event | category | flops | bytes accessed | tf_op | source)
XLA Modules:
  0.0 36.2 jit_solution(16369703465194187234)
XLA Ops:
  0.6 34.7 %shard_map.86 = (f32[6,5]{1,0:T(8,128)S(1)}, f32[6,256,128]{2,1,0:T(8,128)S(1)}) custom-call(f32[8,8]{1,0:T(8,128)} %line.1, f32[8]{0:T(128)} %deriv.1, f32[256,128]{1,0:T(8,128)} %bitcast.4, f32[256,128]{1,0:T(8,128)} %bitcast.5, f32[256,128]{1,0:T(8,128)} %bitcast.6, f32[4,128]{1,0:T(4,128)} %stf.1, s32[4,4,128]{2,1,0:T(4,128)} %wal.1), custom_call_target="tpu_custom_call" | custom-call | tf_op jit(solution)/shard_map/pallas_call | solution.py:572
  35.3 0.9 %shard_map.87 = (f32[6,5]{1,0:T(8,128)}, f32[6,256,128]{2,1,0:T(8,128)}) custom-call(f32[6,5]{1,0:T(8,128)S(1)} %get-tuple-element.6.hess, f32[6,256,128]{2,1,0:T(8,128)S(1)} %get-tuple-element.7.basis), custom_call_target="tpu_custom_call" | custom-call | tf_op jit(solution)/shard_map/pallas_call | solution.py:622
where the time goes:
time: 36.5 us; the launch traced here: 36.2 us
  Pallas kernels  35.6 us (98%)
  between operations  0.64 us (2%)
    pallas_call x1, Pallas kernels, body(): pl.pallas_call(functools.partial(kernel, nx, ny, total), out_shape=(pltpu...  34.7 us
    pallas_call x1, Pallas kernels, body(): pl.pallas_call(store, out_shape=(jax.ShapeDtypeStruct(hess.shape, jnp.flo...  0.9 us

commit v1 on v0

--- a/solution.py
+++ b/solution.py
@@ -15,14 +15,21 @@
 PAIRS = P_SIZE // 2
 SLOT = 32
 GHOST = 8
-WIDE = 3 * P_SIZE + 4
-NARROW = 3 * 2 + 1
+WIDE = 2 * P_SIZE + 4
+NARROW = 2 * 2 + 1
 MESH = pl.DeviceIdType.MESH
 
 
 def block_offsets(nx):
     near = min(nx, 5)
     return list(range(-((near - 1) // 2), near // 2 + 1))
+
+
+def wrapped(o, nx):
+    for same in (o, o - nx, o + nx):
+        if same in block_offsets(nx):
+            return same
+    return None
 
 
 def kernel(
@@ -31,13 +38,13 @@
     hess_out, bas,
     coef, gcoef, scoef, sgcoef, small, src, ini, rea,
     wide, low_send, high_send, south_in, north_in,
-    page_ini, page_src, page_rea, page_small, page_a, page_b, patch,
-    in_sem, hsend, hrecv, rsend, rrecv,
-    hs_sem, hr_sem, ws_sem, wr_sem, ns_sem, nr_sem, rs_sem, rr_sem,
+    page_rea, page_small, page_a, page_b, patch,
+    in_sem, hsend, hrecv, ysend, yrecv, rsend, rrecv,
+    hs_sem, hr_sem, ys_sem, yr_sem, ws_sem, wr_sem, ns_sem, nr_sem, rs_sem, rr_sem,
 ):
     n = nx * ny
     offs = block_offsets(nx)
-    blocks = len(offs)
+    near = [o for o in offs if abs(o) <= 1]
     here = offs.index(0)
     gx, gy = lax.axis_index("gx"), lax.axis_index("gy")
     me = gx * ny + gy
@@ -84,7 +91,6 @@
     slot_of = lane // SLOT
     in_slot = lane % SLOT
     south_half = in_slot < SLOT // 2
-    group_of = in_slot // GHOST
 
     def srl(v, s):
         s = s % 8
@@ -186,8 +192,45 @@
         last = [open_e * jnp.where(xpos == 3, srl(cw, 3 - p), 0.0) for p in range(PAIRS)]
         return first, last
 
-    def operate(get, faces, moved, emit):
+    edge_lane = lane == jnp.where(low, 0, 127)
+
+    def yfaces(get):
+        own, across = [], []
+        for a in range(P_SIZE):
+            vs = [get(a, p) for p in range(PAIRS)]
+            s = dot((gcoef[p], vs[p]) for p in range(PAIRS))
+            t = dot((gcoef[PAIRS + p], vs[p]) for p in range(PAIRS))
+            u = halves(s, t) + srl(halves(t, s), 4)
+            q = srl(u, 4)
+            own.append(u)
+            across.append(halves(lrl(q, 1), lrl(q, 127)))
+        return own, across
+
+    def y_copy(target, device):
+        return pltpu.make_async_remote_copy(
+            src_ref=ysend,
+            dst_ref=yrecv.at[target],
+            send_sem=ys_sem.at[target],
+            recv_sem=yr_sem.at[target],
+            device_id=device,
+            device_id_type=MESH,
+        )
+
+    def y_copies():
+        return [y_copy(0, at(0, 1)), y_copy(1, at(0, -1))]
+
+    def send_yfaces(across):
+        packed = across[0]
+        for a in range(1, P_SIZE):
+            mask = lane == jnp.where(low, a, a - 1)
+            packed = jnp.where(mask, lrl(across[a], a), packed)
+        ysend[...] = packed
+        for copy in y_copies():
+            copy.start()
+
+    def operate(get, faces, given, emit):
         fw, fe = faces
+        own, across = given or yfaces(get)
         stiff, open_w, open_e, open_y = small[0], small[1], small[2], small[3]
         sides = {}
         for p in range(PAIRS):
@@ -198,11 +241,8 @@
         for a in range(P_SIZE):
             vs = [get(a, p) for p in range(PAIRS)]
             ss = [srl(v, 4) for v in vs]
-            s = dot((gcoef[p], vs[p]) for p in range(PAIRS))
-            t = dot((gcoef[PAIRS + p], vs[p]) for p in range(PAIRS))
-            own = halves(s, t) + srl(halves(t, s), 4)
-            q = srl(own, 4)
-            term = own - open_y * halves(lrl(q, 1), lrl(q, 127))
+            beside = jnp.where(edge_lane, 0.0, across[a]) if given else across[a]
+            term = own[a] - open_y * beside
             for p in range(PAIRS):
                 acc = None
                 for r in range(PAIRS):
@@ -210,7 +250,7 @@
                     part = coef[k] * vs[r] + coef[k + 1] * ss[r]
                     acc = part if acc is None else acc + part
                 other = dot((line[a, c], get(c, p)) for c in range(P_SIZE))
-                react = tile(rea, a, p) - shift if moved else tile(rea, a, p)
+                react = tile(rea, a, p) if given else tile(rea, a, p) - shift
                 value = react * vs[p] + stiff * (acc + other)
                 if p == 0:
                     value = value + jnp.where(low, term, 0.0)
@@ -266,66 +306,79 @@
         value = fold(value)
         return lambda k: jnp.broadcast_to(value[:, k:k + 1], (8, 128))
 
-    fields = ((ini, 0), (src, 1), (rea, 2))
-
-    def narrow_copy(sent, held, back, dx, dy):
-        j = offs.index(back)
+    def narrow_copy(late, o, dy):
+        sent, held = (low_send, north_in) if dy < 0 else (high_send, south_in)
+        rows = pl.ds(0, 2) if late else pl.ds(2, 3)
+        j = near.index(wrapped(-o, nx))
+        sems = (1 if late else 0, 0 if dy < 0 else 1, j)
         return pltpu.make_async_remote_copy(
-            src_ref=sent,
-            dst_ref=held.at[j],
-            send_sem=ns_sem.at[0 if dy < 0 else 1, j],
-            recv_sem=nr_sem.at[0 if dy < 0 else 1, j],
-            device_id=at(dx, dy),
+            src_ref=sent.at[rows],
+            dst_ref=held.at[j, rows],
+            send_sem=ns_sem.at[sems],
+            recv_sem=nr_sem.at[sems],
+            device_id=at(o, dy),
             device_id_type=MESH,
         )
 
-    def opposite(o):
-        return -o if -o in offs else o
-
-    def wide_copy(o):
-        j = offs.index(opposite(o))
+    def wide_copy(late, o):
+        rows = pl.ds(0, P_SIZE) if late else pl.ds(P_SIZE, P_SIZE + 4)
+        j = offs.index(wrapped(-o, nx))
+        sems = (1 if late else 0, j)
         return pltpu.make_async_remote_copy(
-            src_ref=wide.at[here],
-            dst_ref=wide.at[j],
-            send_sem=ws_sem.at[j],
-            recv_sem=wr_sem.at[j],
+            src_ref=wide.at[here, rows],
+            dst_ref=wide.at[j, rows],
+            send_sem=ws_sem.at[sems],
+            recv_sem=wr_sem.at[sems],
             device_id=at(o, 0),
             device_id_type=MESH,
         )
 
-    def pack_edges():
-        def gathered(parts):
-            return by_slot([lrl(parts[p], 16 + SLOT * p) for p in range(PAIRS)])
-
-        def narrow(items, index):
-            for ref, start in ((low_send, 16), (high_send, 8)):
-                out = None
-                for i, v in enumerate(items):
-                    moved = lrl(v, GHOST * i - start)
-                    out = moved if out is None else jnp.where(group_of == i, moved, out)
-                ref[index] = out
-
-        for ref, f in fields:
-            for quad in range(2):
-                items = []
-                for a in range(4 * quad, 4 * quad + 4):
-                    v = gathered([tile(ref, a, p) for p in range(PAIRS)])
-                    wide[here, f * P_SIZE + a] = v
-                    items.append(v)
-                narrow(items, f * 2 + quad)
+    def strip_copies(late):
+        return [narrow_copy(late, o, dy) for dy in (-1, 1) for o in near] + [
+            wide_copy(late, o) for o in sorted(offs, key=abs) if o
+        ]
+
+    def gathered(parts):
+        return by_slot([lrl(parts[p], 16 + SLOT * p) for p in range(PAIRS)])
+
+    def pack_narrow(items, index):
+        for ref, start in ((low_send, 16), (high_send, 8)):
+            out = None
+            for i, v in enumerate(items):
+                moved = lrl(v, GHOST * i - start)
+                out = moved if out is None else jnp.where(in_slot // GHOST == i, moved, out)
+            ref[index] = out
+
+    def pack_field(ref, wide_at, narrow_at):
+        for quad in range(2):
+            items = []
+            for a in range(4 * quad, 4 * quad + 4):
+                v = gathered([tile(ref, a, p) for p in range(PAIRS)])
+                wide[here, wide_at + a] = v
+                items.append(v)
+            pack_narrow(items, narrow_at + quad)
+
+    def pack_small():
         items = []
         for f in range(4):
             v = gathered([small[f]] * PAIRS)
-            wide[here, 3 * P_SIZE + f] = v
+            wide[here, 2 * P_SIZE + f] = v
             items.append(v)
-        narrow(items, 6)
-
-    narrow_copies = [
-        narrow_copy(low_send, north_in, opposite(o), o, -1) for o in offs
-    ] + [
-        narrow_copy(high_send, south_in, opposite(o), o, 1) for o in offs
-    ]
-    wide_copies = [wide_copy(o) for o in sorted(offs, key=abs) if o]
+        pack_narrow(items, 4)
+
+    def finish_first():
+        for copy in y_copies():
+            copy.wait_recv()
+        cy = halves(yrecv[0], yrecv[1])
+        first = bas.at[0]
+        for a in range(P_SIZE):
+            term = small[3] * jnp.where(edge_lane, lrl(cy, -a), 0.0)
+            put(first, a, 0, tile(first, a, 0) + jnp.where(low, term, 0.0))
+            last = PAIRS - 1
+            put(first, a, last, tile(first, a, last) + jnp.where(low, 0.0, term))
+        pack_field(first, 0, 0)
+        for copy in strip_copies(True):
+            copy.start()
 
     for d in range(PAIRS):
         for k in range(2):
@@ -335,41 +388,50 @@
     y_mask = (low & (slot_of == 0)) | (~low & (slot_of == PAIRS - 1))
 
     def unpack_pages():
-        def merge(seam, wide_part, narrow_part, i):
+        def merge(seam, o, wide_at, narrow_at, i):
+            wide_part = wide[offs.index(o), wide_at]
+            if o not in near:
+                return wide_part
+            narrow_part = (south_in, north_in)[seam][near.index(o), narrow_at]
             if seam == 0:
                 return jnp.where(south_half, lrl(narrow_part, GHOST - GHOST * i), wide_part)
             return jnp.where(south_half, wide_part, lrl(narrow_part, 16 - GHOST * i))
 
-        for seam, narrow_in in ((0, south_in), (1, north_in)):
-            for j in range(blocks):
-                for f, page in enumerate((page_ini, page_src, page_rea)):
-                    for a in range(P_SIZE):
-                        page[seam, j * P_SIZE + a] = merge(
-                            seam, wide[j, f * P_SIZE + a], narrow_in[j, f * 2 + a // 4], a % 4
+        for seam in range(2):
+            for j, o in enumerate(offs):
+                for a in range(P_SIZE):
+                    page_a[seam, j * P_SIZE + a] = merge(seam, o, a, a // 4, a % 4)
+                    if o in near:
+                        page_rea[seam, j * P_SIZE + a] = (
+                            merge(seam, o, P_SIZE + a, 2 + a // 4, a % 4) - shift
                         )
-                for f in range(4):
-                    page_small[seam, j * 4 + f] = merge(
-                        seam, wide[j, 3 * P_SIZE + f], narrow_in[j, 6], f
-                    )
+                if o in near:
+                    for f in range(4):
+                        page_small[seam, j * 4 + f] = merge(seam, o, 2 * P_SIZE + f, 4, f)
 
     def page_level(level):
-        given = page_ini if level == 0 else (page_a if level % 2 else page_b)
-        out = page_b if level % 2 else page_a
-
-        def seam_body(seam, carry):
-            fw, fe = [], []
-            for j in range(blocks):
-                vs = [given[seam, j * P_SIZE + a] for a in range(P_SIZE)]
-                fw.append(dot(zip(glow, vs)))
-                fe.append(dot(zip(gupp, vs)))
-            for j in range(blocks):
+        given, out = (page_a, page_b) if level % 2 else (page_b, page_a)
+        targets = near if level < ITERS else [0]
+
+        def known(o):
+            o = wrapped(o, nx)
+            return o is not None and (level == 1 or o in near)
+
+        for seam in range(2):
+            def face(weights, o):
+                j = offs.index(wrapped(o, nx)) * P_SIZE
+                return dot((weights[a], given[seam, j + a]) for a in range(P_SIZE))
+
+            for o in targets:
+                j = offs.index(o)
                 stiff, open_w, open_e, open_y = [page_small[seam, j * 4 + f] for f in range(4)]
-                nb_e = jnp.where(xpos == 3, srl(fw[(j + 1) % blocks], 3), srl(fw[j], 7))
-                nb_w = jnp.where(xpos == 0, srl(fe[(j - 1) % blocks], 5), srl(fe[j], 1))
-                sides = {
-                    0: fw[j] - open_w * nb_w,
-                    P_SIZE - 1: fe[j] - open_e * nb_e,
-                }
+                fw, fe = face(glow, o), face(gupp, o)
+                nb_e, nb_w = srl(fw, 7), srl(fe, 1)
+                if known(o + 1):
+                    nb_e = jnp.where(xpos == 3, srl(face(glow, o + 1), 3), nb_e)
+                if known(o - 1):
+                    nb_w = jnp.where(xpos == 0, srl(face(gupp, o - 1), 5), nb_w)
+                sides = {0: fw - open_w * nb_w, P_SIZE - 1: fe - open_e * nb_e}
                 vs = [given[seam, j * P_SIZE + a] for a in range(P_SIZE)]
                 for a in range(P_SIZE):
                     v = vs[a]
@@ -379,23 +441,15 @@
                         acc = acc + lrl(scoef[2 * d] * v + scoef[2 * d + 1] * ss, SLOT * d)
                     s, t = sgcoef[0] * v, sgcoef[1] * v
                     own = halves(s, t) + srl(halves(t, s), 4)
-                    own = own + lrl(own, 64)
-                    own = own + lrl(own, 32)
+                    own = (own + lrl(own, 64)) + (lrl(own, 32) + lrl(own, 96))
                     q = srl(own, 4)
                     term = own - open_y * halves(lrl(q, 1), lrl(q, 127))
                     other = dot(zip([line[a, c] for c in range(P_SIZE)], vs))
-                    react = page_rea[seam, j * P_SIZE + a]
-                    if level:
-                        react = react - shift
-                    value = react * v + stiff * (acc + other) + jnp.where(y_mask, term, 0.0)
+                    value = page_rea[seam, j * P_SIZE + a] * v + stiff * (acc + other)
+                    value = value + jnp.where(y_mask, term, 0.0)
                     if a in sides:
                         value = value + sides[a]
-                    if level == 0:
-                        value = page_src[seam, j * P_SIZE + a] - value
                     out[seam, j * P_SIZE + a] = value
-            return carry
-
-        lax.fori_loop(0, 2, seam_body, 0)
         for a in range(P_SIZE):
             k = here * P_SIZE + a
             patch[level, a] = jnp.where(south_half, out[1, k], out[0, k])
@@ -403,6 +457,8 @@
     edge = (lane < VECS) | (lane >= 128 - VECS)
 
     def patched(level, a, p, v):
+        if level == 0:
+            return v
         return jnp.where(edge, lrl(patch[level, a], 112 - SLOT * p), v)
 
     started = []
@@ -412,15 +468,17 @@
     faces = xfaces(get)
     copies = send_halo(0, faces, lambda: pl.semaphore_wait(barrier, n - 1))
     started += copies
+    given = yfaces(get)
+    send_yfaces(given[1])
     loads[1].wait()
     loads[2].wait()
-    y0 = bas.at[0]
-    operate(get, faces, False, lambda a, p, v: put(y0, a, p, tile(src, a, p) - v))
-    pack_edges()
-    for copy in narrow_copies:
+    operate(get, faces, given, lambda a, p, v: put(bas.at[0], a, p, tile(src, a, p) - v))
+    pack_field(rea, P_SIZE, 2)
+    pack_small()
+    for copy in strip_copies(False):
         copy.start()
 
-    ways = len(wide_copies)
+    late = gy == ny - 1
     for level in range(ITERS):
         now = bas.at[level]
         get = functools.partial(tile, now)
@@ -433,13 +491,11 @@
         for p in range(PAIRS):
             put(now, 0, p, get(0, p) + first[p])
             put(now, P_SIZE - 1, p, get(P_SIZE - 1, p) + last[p])
-        operate(get, (fw, fe), True, functools.partial(put, bas.at[level + 1]))
+        operate(get, (fw, fe), None, functools.partial(put, bas.at[level + 1]))
         if level == 0:
-            for copy in wide_copies[:ways - ways // 2]:
-                copy.start()
+            pl.when(jnp.logical_not(late))(finish_first)
         if level == 1:
-            for copy in wide_copies[ways - ways // 2:]:
-                copy.start()
+            pl.when(late)(finish_first)
             accs = [None] * 3
             for a, p in tiles():
                 u, v = tile(bas.at[0], a, p), tile(bas.at[1], a, p)
@@ -447,11 +503,11 @@
                 accs = new if accs[0] is None else [s + t for s, t in zip(accs, new)]
             start_reduce(0, pack_sums(accs, 0))
         if level == 3:
-            for copy in narrow_copies + wide_copies:
+            for copy in strip_copies(False) + strip_copies(True):
                 copy.wait_recv()
             unpack_pages()
-            for k in range(3):
-                page_level(k)
+            page_level(1)
+            page_level(2)
         if level == 4:
             for k in range(3, VECS):
                 page_level(k)
@@ -536,7 +592,7 @@
             put(bas.at[j], a, p, dot(zip(combos[j], vecs)))
     hess_out[...] = hess[0:VECS, 0:ITERS]
 
-    for copy in started + narrow_copies + wide_copies:
+    for copy in started + y_copies() + strip_copies(False) + strip_copies(True):
         copy.wait_send()
     for slot in range(2):
         block = rrecv.at[slot, pl.ds(0, n - 1)]
@@ -559,7 +615,9 @@
     n = nx * ny
     rows = nodes * ex
     flat = (rows, ey)
-    blocks = len(block_offsets(nx))
+    offs = block_offsets(nx)
+    blocks = len(offs)
+    near = len([o for o in offs if abs(o) <= 1])
     total = float(nodes * ex * nx * ey * ny)
     vmem = pl.BlockSpec(memory_space=pltpu.VMEM)
     hbm = pl.BlockSpec(memory_space=pl.ANY)
@@ -589,10 +647,8 @@
             array(blocks, WIDE),
             array(NARROW),
             array(NARROW),
-            array(blocks, NARROW),
-            array(blocks, NARROW),
-            array(2, blocks * P_SIZE),
-            array(2, blocks * P_SIZE),
+            array(near, NARROW),
+            array(near, NARROW),
             array(2, blocks * P_SIZE),
             array(2, blocks * 4),
             array(2, blocks * P_SIZE),
@@ -601,14 +657,18 @@
             dma((3,)),
             array(VECS, 2),
             array(VECS, 2),
+            array(),
+            array(2),
             pltpu.VMEM((2, 1, 128), jnp.float32),
             pltpu.VMEM((2, n, 128), jnp.float32),
             dma((VECS, 2)),
             dma((VECS, 2)),
-            dma((blocks,)),
-            dma((blocks,)),
+            dma((2,)),
+            dma((2,)),
             dma((2, blocks)),
             dma((2, blocks)),
+            dma((2, 2, near)),
+            dma((2, 2, near)),
             dma((2,)),
             dma((2,)),
         ],

time: 36.5 us -> 38.3 us (1.049)
  Pallas kernels: 35.6 us -> 37.5 us
    pallas_call x1, Pallas kernels: 34.7 us -> 36.6 us  [body(): pl.pallas_call(functools.partial(kernel, nx, ny, total), out_shape=(pltpu...]
where the time goes in v1:
time: 38.3 us; the launch traced here: 38.1 us
  Pallas kernels  37.5 us (98%)
  between operations  0.64 us (2%)
    pallas_call x1, Pallas kernels, body(): pl.pallas_call(functools.partial(kernel, nx, ny, total), out_shape=(pltpu...  36.6 us
    pallas_call x1, Pallas kernels, body(): pl.pallas_call(store, out_shape=(jax.ShapeDtypeStruct(hess.shape, jnp.flo...  0.9 us

profile of v1, /device:TPU:0, one launch (start us, length us, event | category | flops | bytes accessed | tf_op | source)
XLA Modules:
  0.0 38.1 jit_solution(14991137361377145058)
XLA Ops:
  0.6 36.6 %shard_map.86 = (f32[6,5]{1,0:T(8,128)S(1)}, f32[6,256,128]{2,1,0:T(8,128)S(1)}) custom-call(f32[8,8]{1,0:T(8,128)} %line.1, f32[8]{0:T(128)} %deriv.1, f32[256,128]{1,0:T(8,128)} %bitcast.4, f32[256,128]{1,0:T(8,128)} %bitcast.5, f32[256,128]{1,0:T(8,128)} %bitcast.6, f32[4,128]{1,0:T(4,128)} %stf.1, s32[4,4,128]{2,1,0:T(4,128)} %wal.1), custom_call_target="tpu_custom_call" | custom-call | tf_op jit(solution)/shard_map/pallas_call | solution.py:630
  37.2 0.9 %shard_map.87 = (f32[6,5]{1,0:T(8,128)}, f32[6,256,128]{2,1,0:T(8,128)}) custom-call(f32[6,5]{1,0:T(8,128)S(1)} %get-tuple-element.6.hess, f32[6,256,128]{2,1,0:T(8,128)S(1)} %get-tuple-element.7.basis), custom_call_target="tpu_custom_call" | custom-call | tf_op jit(solution)/shard_map/pallas_call | solution.py:682

commit v2 on v1

--- a/solution.py
+++ b/solution.py
@@ -13,39 +13,26 @@
 TAU = 2.0
 FLOOR = 0.1
 PAIRS = P_SIZE // 2
-SLOT = 32
-GHOST = 8
-WIDE = 2 * P_SIZE + 4
-NARROW = 2 * 2 + 1
+SLOT = 16
+GHOSTS = ITERS
+OWNED = SLOT - GHOSTS
+WIDE = 2 * P_SIZE + 1
+NARROW = P_SIZE + 1
 MESH = pl.DeviceIdType.MESH
-
-
-def block_offsets(nx):
-    near = min(nx, 5)
-    return list(range(-((near - 1) // 2), near // 2 + 1))
-
-
-def wrapped(o, nx):
-    for same in (o, o - nx, o + nx):
-        if same in block_offsets(nx):
-            return same
-    return None
 
 
 def kernel(
     nx, ny, total,
     line, deriv, src_any, ini_any, rea_any, stf, wal,
     hess_out, bas,
-    coef, gcoef, scoef, sgcoef, small, src, ini, rea,
-    wide, low_send, high_send, south_in, north_in,
+    coef, gcoef, small, src, ini, rea,
+    wide, narrow, narrow_in, far_send, far_in,
     page_rea, page_small, page_a, page_b, patch,
     in_sem, hsend, hrecv, ysend, yrecv, rsend, rrecv,
-    hs_sem, hr_sem, ys_sem, yr_sem, ws_sem, wr_sem, ns_sem, nr_sem, rs_sem, rr_sem,
+    hs_sem, hr_sem, ys_sem, yr_sem, ws_sem, wr_sem, ns_sem, nr_sem,
+    fs_sem, fr_sem, rs_sem, rr_sem,
 ):
     n = nx * ny
-    offs = block_offsets(nx)
-    near = [o for o in offs if abs(o) <= 1]
-    here = offs.index(0)
     gx, gy = lax.axis_index("gx"), lax.axis_index("gy")
     me = gx * ny + gy
 
@@ -88,10 +75,6 @@
     lane = lax.broadcasted_iota(jnp.int32, (8, 128), 1)
     low = sub < 4
     xpos = sub % 4
-    slot_of = lane // SLOT
-    in_slot = lane % SLOT
-    south_half = in_slot < SLOT // 2
-
     def srl(v, s):
         s = s % 8
         return v if s == 0 else pltpu.roll(v, s, 0)
@@ -103,10 +86,13 @@
     def halves(a, b):
         return jnp.where(low, a, b)
 
-    def by_slot(parts):
-        out = parts[0]
-        for p in range(1, PAIRS):
-            out = jnp.where(slot_of == p, parts[p], out)
+    def within(start, count):
+        return (lane >= start) & (lane < start + count)
+
+    def overlay(parts):
+        out = None
+        for mask, v in parts:
+            out = v if out is None else jnp.where(mask, v, out)
         return out
 
     def dot(pairs):
@@ -115,22 +101,18 @@
             out = c * v if out is None else out + c * v
         return out
 
-    mix = {}
     for p in range(PAIRS):
         for r in range(PAIRS):
-            mix[p, r, 0] = halves(line[2 * p, 2 * r], line[2 * p + 1, 2 * r + 1])
-            mix[p, r, 1] = halves(line[2 * p, 2 * r + 1], line[2 * p + 1, 2 * r])
-            for k in range(2):
-                coef[(p * PAIRS + r) * 2 + k] = mix[p, r, k]
+            k = (p * PAIRS + r) * 2
+            coef[k] = halves(line[2 * p, 2 * r], line[2 * p + 1, 2 * r + 1])
+            coef[k + 1] = halves(line[2 * p, 2 * r + 1], line[2 * p + 1, 2 * r])
     glow = [0.5 * deriv[c] + (TAU if c == 0 else 0.0) for c in range(P_SIZE)]
     gupp = [
         0.5 * deriv[P_SIZE - 1 - c] + (TAU if c == P_SIZE - 1 else 0.0) for c in range(P_SIZE)
     ]
-    lows = [halves(glow[2 * p], glow[2 * p + 1]) for p in range(PAIRS)]
-    upps = [halves(gupp[2 * p], gupp[2 * p + 1]) for p in range(PAIRS)]
     for p in range(PAIRS):
-        gcoef[p] = lows[p]
-        gcoef[PAIRS + p] = upps[p]
+        gcoef[p] = halves(glow[2 * p], glow[2 * p + 1])
+        gcoef[PAIRS + p] = halves(gupp[2 * p], gupp[2 * p + 1])
     small[0, 0:4] = stf[...]
     small[0, 4:8] = stf[...]
     opened = [1.0 - wal[f].astype(jnp.float32) for f in range(4)]
@@ -169,12 +151,16 @@
             device_id_type=MESH,
         )
 
-    def send_halo(slot, faces, ready=lambda: None):
+    def pack_faces(faces):
         fw, fe = faces
         cw, ce = fw[0], srl(fe[0], -3)
         for p in range(1, PAIRS):
             cw = jnp.where(xpos == p, srl(fw[p], p), cw)
             ce = jnp.where(xpos == p, srl(fe[p], p - 3), ce)
+        return cw, ce
+
+    def send_halo(slot, faces, ready=lambda: None):
+        cw, ce = pack_faces(faces)
         hsend[slot, 0] = cw
         hsend[slot, 1] = ce
         ready()
@@ -228,21 +214,12 @@
         for copy in y_copies():
             copy.start()
 
-    def operate(get, faces, given, emit):
-        fw, fe = faces
-        own, across = given or yfaces(get)
-        stiff, open_w, open_e, open_y = small[0], small[1], small[2], small[3]
-        sides = {}
-        for p in range(PAIRS):
-            nb_e = jnp.where(xpos == 3, 0.0, srl(fw[p], 7))
-            nb_w = jnp.where(xpos == 0, 0.0, srl(fe[p], 1))
-            sides[0, p] = fw[p] - open_w * nb_w
-            sides[P_SIZE - 1, p] = fe[p] - open_e * nb_e
+    def apply(get, react, fields, sides, own, across, emit):
+        stiff, open_w, open_e, open_y = fields
         for a in range(P_SIZE):
             vs = [get(a, p) for p in range(PAIRS)]
             ss = [srl(v, 4) for v in vs]
-            beside = jnp.where(edge_lane, 0.0, across[a]) if given else across[a]
-            term = own[a] - open_y * beside
+            term = own[a] - open_y * across[a]
             for p in range(PAIRS):
                 acc = None
                 for r in range(PAIRS):
@@ -250,8 +227,7 @@
                     part = coef[k] * vs[r] + coef[k + 1] * ss[r]
                     acc = part if acc is None else acc + part
                 other = dot((line[a, c], get(c, p)) for c in range(P_SIZE))
-                react = tile(rea, a, p) if given else tile(rea, a, p) - shift
-                value = react * vs[p] + stiff * (acc + other)
+                value = react(a, p) * vs[p] + stiff * (acc + other)
                 if p == 0:
                     value = value + jnp.where(low, term, 0.0)
                 if p == PAIRS - 1:
@@ -259,6 +235,23 @@
                 if (a, p) in sides:
                     value = value + sides[a, p]
                 emit(a, p, value)
+
+    def operate(get, faces, given, emit):
+        fw, fe = faces
+        fields = [small[f] for f in range(4)]
+        sides = {}
+        for p in range(PAIRS):
+            nb_e = jnp.where(xpos == 3, 0.0, srl(fw[p], 7))
+            nb_w = jnp.where(xpos == 0, 0.0, srl(fe[p], 1))
+            sides[0, p] = fw[p] - fields[1] * nb_w
+            sides[P_SIZE - 1, p] = fe[p] - fields[2] * nb_e
+        own, across = given or yfaces(get)
+        if given:
+            across = [jnp.where(edge_lane, 0.0, v) for v in across]
+            react = functools.partial(tile, rea)
+        else:
+            react = lambda a, p: tile(rea, a, p) - shift
+        apply(get, react, fields, sides, own, across, emit)
 
     def gather_rows(accs):
         zero = jnp.zeros((8, 128), jnp.float32)
@@ -306,14 +299,15 @@
         value = fold(value)
         return lambda k: jnp.broadcast_to(value[:, k:k + 1], (8, 128))
 
+    near = (-1, 0, 1)
+
     def narrow_copy(late, o, dy):
-        sent, held = (low_send, north_in) if dy < 0 else (high_send, south_in)
-        rows = pl.ds(0, 2) if late else pl.ds(2, 3)
-        j = near.index(wrapped(-o, nx))
-        sems = (1 if late else 0, 0 if dy < 0 else 1, j)
+        rows = pl.ds(0, PAIRS) if late else pl.ds(PAIRS, PAIRS + 1)
+        side, j = (0 if dy > 0 else 1), near.index(-o)
+        sems = (1 if late else 0, side, j)
         return pltpu.make_async_remote_copy(
-            src_ref=sent.at[rows],
-            dst_ref=held.at[j, rows],
+            src_ref=narrow.at[rows],
+            dst_ref=narrow_in.at[side, j, rows],
             send_sem=ns_sem.at[sems],
             recv_sem=nr_sem.at[sems],
             device_id=at(o, dy),
@@ -321,11 +315,11 @@
         )
 
     def wide_copy(late, o):
-        rows = pl.ds(0, P_SIZE) if late else pl.ds(P_SIZE, P_SIZE + 4)
-        j = offs.index(wrapped(-o, nx))
+        rows = pl.ds(0, P_SIZE) if late else pl.ds(P_SIZE, P_SIZE + 1)
+        j = near.index(-o)
         sems = (1 if late else 0, j)
         return pltpu.make_async_remote_copy(
-            src_ref=wide.at[here, rows],
+            src_ref=wide.at[1, rows],
             dst_ref=wide.at[j, rows],
             send_sem=ws_sem.at[sems],
             recv_sem=wr_sem.at[sems],
@@ -333,38 +327,51 @@
             device_id_type=MESH,
         )
 
+    def far_copy(way, o):
+        return pltpu.make_async_remote_copy(
+            src_ref=far_send.at[way],
+            dst_ref=far_in.at[way],
+            send_sem=fs_sem.at[way],
+            recv_sem=fr_sem.at[way],
+            device_id=at(o, 0),
+            device_id_type=MESH,
+        )
+
     def strip_copies(late):
-        return [narrow_copy(late, o, dy) for dy in (-1, 1) for o in near] + [
-            wide_copy(late, o) for o in sorted(offs, key=abs) if o
-        ]
-
-    def gathered(parts):
-        return by_slot([lrl(parts[p], 16 + SLOT * p) for p in range(PAIRS)])
-
-    def pack_narrow(items, index):
-        for ref, start in ((low_send, 16), (high_send, 8)):
-            out = None
-            for i, v in enumerate(items):
-                moved = lrl(v, GHOST * i - start)
-                out = moved if out is None else jnp.where(in_slot // GHOST == i, moved, out)
-            ref[index] = out
+        copies = [narrow_copy(late, o, dy) for dy in (-1, 1) for o in near]
+        copies += [wide_copy(late, o) for o in (-1, 1)]
+        if late:
+            copies += [far_copy(0, -2), far_copy(1, 2)]
+        return copies
+
+    def pack_wide(items, index):
+        parts = []
+        for p, v in enumerate(items):
+            parts.append((within(32 * p, SLOT), lrl(v, 32 * p)))
+            spot = (32 * p + 48) % 128
+            parts.append((within(spot, SLOT), lrl(v, spot - (128 - OWNED))))
+        wide[1, index] = overlay(parts)
+
+    def pack_narrow(pairs, index):
+        parts = []
+        for i, items in enumerate(pairs):
+            for p, v in enumerate(items):
+                spot = SLOT * p + 8 * i
+                parts.append((within(spot, 8), lrl(v, spot - (128 - GHOSTS))))
+                parts.append((within(64 + spot, 8), lrl(v, 64 + spot)))
+        narrow[index] = overlay(parts)
 
     def pack_field(ref, wide_at, narrow_at):
-        for quad in range(2):
-            items = []
-            for a in range(4 * quad, 4 * quad + 4):
-                v = gathered([tile(ref, a, p) for p in range(PAIRS)])
-                wide[here, wide_at + a] = v
-                items.append(v)
-            pack_narrow(items, narrow_at + quad)
+        rows = [[tile(ref, a, p) for p in range(PAIRS)] for a in range(P_SIZE)]
+        for a in range(P_SIZE):
+            pack_wide(rows[a], wide_at + a)
+        for q in range(PAIRS):
+            pack_narrow(rows[2 * q:2 * q + 2], narrow_at + q)
 
     def pack_small():
-        items = []
-        for f in range(4):
-            v = gathered([small[f]] * PAIRS)
-            wide[here, 2 * P_SIZE + f] = v
-            items.append(v)
-        pack_narrow(items, 4)
+        items = [small[f] for f in range(4)]
+        pack_wide(items, 2 * P_SIZE)
+        pack_narrow([items], 2 * PAIRS)
 
     def finish_first():
         for copy in y_copies():
@@ -376,90 +383,74 @@
             put(first, a, 0, tile(first, a, 0) + jnp.where(low, term, 0.0))
             last = PAIRS - 1
             put(first, a, last, tile(first, a, last) + jnp.where(low, 0.0, term))
+        cw, ce = pack_faces(xfaces(functools.partial(tile, first)))
+        far_send[0] = cw
+        far_send[1] = ce
         pack_field(first, 0, 0)
         for copy in strip_copies(True):
             copy.start()
 
-    for d in range(PAIRS):
-        for k in range(2):
-            scoef[2 * d + k] = by_slot([mix[(r + d) % PAIRS, r, k] for r in range(PAIRS)])
-    sgcoef[0] = by_slot(lows)
-    sgcoef[1] = by_slot(upps)
-    y_mask = (low & (slot_of == 0)) | (~low & (slot_of == PAIRS - 1))
-
-    def unpack_pages():
-        def merge(seam, o, wide_at, narrow_at, i):
-            wide_part = wide[offs.index(o), wide_at]
-            if o not in near:
-                return wide_part
-            narrow_part = (south_in, north_in)[seam][near.index(o), narrow_at]
-            if seam == 0:
-                return jnp.where(south_half, lrl(narrow_part, GHOST - GHOST * i), wide_part)
-            return jnp.where(south_half, wide_part, lrl(narrow_part, 16 - GHOST * i))
-
-        for seam in range(2):
-            for j, o in enumerate(offs):
-                for a in range(P_SIZE):
-                    page_a[seam, j * P_SIZE + a] = merge(seam, o, a, a // 4, a % 4)
-                    if o in near:
-                        page_rea[seam, j * P_SIZE + a] = (
-                            merge(seam, o, P_SIZE + a, 2 + a // 4, a % 4) - shift
-                        )
-                if o in near:
-                    for f in range(4):
-                        page_small[seam, j * 4 + f] = merge(seam, o, 2 * P_SIZE + f, 4, f)
+    def unpack(wide_at, narrow_at, i, p):
+        parts = []
+        for j in range(3):
+            mask = within(SLOT * (j + 1), OWNED) | within(64 + SLOT * j, OWNED)
+            parts.append((mask, lrl(wide[j, wide_at], SLOT * (j + 1) - 32 * p)))
+        for j in range(3):
+            spot = SLOT * j + OWNED
+            both = jnp.where(lane < 64, narrow_in[0, j, narrow_at], narrow_in[1, j, narrow_at])
+            mask = within(spot, GHOSTS) | within(64 + spot, GHOSTS)
+            parts.append((mask, lrl(both, spot - SLOT * p - 8 * i)))
+        return overlay(parts)
+
+    def unpack_early():
+        for a, p in tiles():
+            value = unpack(P_SIZE + a, PAIRS + a // 2, a % 2, p)
+            put(page_rea, a, p, value - shift)
+        for f in range(4):
+            page_small[f] = unpack(2 * P_SIZE, 2 * PAIRS, 0, f)
+
+    def unpack_late():
+        for a, p in tiles():
+            put(page_a, a, p, unpack(a, a // 2, a % 2, p))
 
     def page_level(level):
         given, out = (page_a, page_b) if level % 2 else (page_b, page_a)
-        targets = near if level < ITERS else [0]
-
-        def known(o):
-            o = wrapped(o, nx)
-            return o is not None and (level == 1 or o in near)
-
-        for seam in range(2):
-            def face(weights, o):
-                j = offs.index(wrapped(o, nx)) * P_SIZE
-                return dot((weights[a], given[seam, j + a]) for a in range(P_SIZE))
-
-            for o in targets:
-                j = offs.index(o)
-                stiff, open_w, open_e, open_y = [page_small[seam, j * 4 + f] for f in range(4)]
-                fw, fe = face(glow, o), face(gupp, o)
-                nb_e, nb_w = srl(fw, 7), srl(fe, 1)
-                if known(o + 1):
-                    nb_e = jnp.where(xpos == 3, srl(face(glow, o + 1), 3), nb_e)
-                if known(o - 1):
-                    nb_w = jnp.where(xpos == 0, srl(face(gupp, o - 1), 5), nb_w)
-                sides = {0: fw - open_w * nb_w, P_SIZE - 1: fe - open_e * nb_e}
-                vs = [given[seam, j * P_SIZE + a] for a in range(P_SIZE)]
-                for a in range(P_SIZE):
-                    v = vs[a]
-                    ss = srl(v, 4)
-                    acc = scoef[0] * v + scoef[1] * ss
-                    for d in range(1, PAIRS):
-                        acc = acc + lrl(scoef[2 * d] * v + scoef[2 * d + 1] * ss, SLOT * d)
-                    s, t = sgcoef[0] * v, sgcoef[1] * v
-                    own = halves(s, t) + srl(halves(t, s), 4)
-                    own = (own + lrl(own, 64)) + (lrl(own, 32) + lrl(own, 96))
-                    q = srl(own, 4)
-                    term = own - open_y * halves(lrl(q, 1), lrl(q, 127))
-                    other = dot(zip([line[a, c] for c in range(P_SIZE)], vs))
-                    value = page_rea[seam, j * P_SIZE + a] * v + stiff * (acc + other)
-                    value = value + jnp.where(y_mask, term, 0.0)
-                    if a in sides:
-                        value = value + sides[a]
-                    out[seam, j * P_SIZE + a] = value
-        for a in range(P_SIZE):
-            k = here * P_SIZE + a
-            patch[level, a] = jnp.where(south_half, out[1, k], out[0, k])
+        get = functools.partial(tile, given)
+        fields = [page_small[f] for f in range(4)]
+        fw, fe = xfaces(get)
+        if level == 1:
+            cw, ce = far_in[0], far_in[1]
+            skip = 128 - OWNED
+            east = jnp.where(lane < 64, lrl(cw, 3 * SLOT), lrl(cw, 6 * SLOT - skip))
+            west = jnp.where(lane < 64, lrl(ce, SLOT), lrl(ce, 4 * SLOT - skip))
+            last = within(2 * SLOT + OWNED, SLOT) | within(6 * SLOT, SLOT)
+            first = within(OWNED, SLOT) | within(4 * SLOT, SLOT)
+        sides = {}
+        for p in range(PAIRS):
+            e, w = lrl(srl(fw[p], 3), -SLOT), lrl(srl(fe[p], 5), SLOT)
+            if level == 1:
+                e = jnp.where(last, srl(east, 3 - p), e)
+                w = jnp.where(first, srl(west, -p), w)
+            nb_e = jnp.where(xpos == 3, e, srl(fw[p], 7))
+            nb_w = jnp.where(xpos == 0, w, srl(fe[p], 1))
+            sides[0, p] = fw[p] - fields[1] * nb_w
+            sides[P_SIZE - 1, p] = fe[p] - fields[2] * nb_e
+        own, across = yfaces(get)
+
+        def emit(a, p, value):
+            put(out, a, p, value)
+            south = lrl(value, -2 * SLOT)
+            north = lrl(value, 128 - OWNED - 5 * SLOT)
+            patch[level - 1, a * PAIRS + p] = jnp.where(lane < 64, south, north)
+
+        apply(get, functools.partial(tile, page_rea), fields, sides, own, across, emit)
 
     edge = (lane < VECS) | (lane >= 128 - VECS)
 
     def patched(level, a, p, v):
         if level == 0:
             return v
-        return jnp.where(edge, lrl(patch[level, a], 112 - SLOT * p), v)
+        return jnp.where(edge, patch[level - 1, a * PAIRS + p], v)
 
     started = []
 
@@ -473,7 +464,7 @@
     loads[1].wait()
     loads[2].wait()
     operate(get, faces, given, lambda a, p, v: put(bas.at[0], a, p, tile(src, a, p) - v))
-    pack_field(rea, P_SIZE, 2)
+    pack_field(rea, P_SIZE, PAIRS)
     pack_small()
     for copy in strip_copies(False):
         copy.start()
@@ -502,14 +493,18 @@
                 new = [u * u, u * v, v * v]
                 accs = new if accs[0] is None else [s + t for s, t in zip(accs, new)]
             start_reduce(0, pack_sums(accs, 0))
+        if level == 2:
+            for copy in strip_copies(False):
+                copy.wait_recv()
+            unpack_early()
         if level == 3:
-            for copy in strip_copies(False) + strip_copies(True):
+            for copy in strip_copies(True):
                 copy.wait_recv()
-            unpack_pages()
-            page_level(1)
-            page_level(2)
+            unpack_late()
+            for k in (1, 2, 3):
+                page_level(k)
         if level == 4:
-            for k in range(3, VECS):
+            for k in (4, 5):
                 page_level(k)
 
     sums = end_reduce(0)
@@ -615,9 +610,6 @@
     n = nx * ny
     rows = nodes * ex
     flat = (rows, ey)
-    offs = block_offsets(nx)
-    blocks = len(offs)
-    near = len([o for o in offs if abs(o) <= 1])
     total = float(nodes * ex * nx * ey * ny)
     vmem = pl.BlockSpec(memory_space=pltpu.VMEM)
     hbm = pl.BlockSpec(memory_space=pl.ANY)
@@ -638,22 +630,20 @@
         scratch_shapes=[
             array(2 * PAIRS * PAIRS),
             array(2 * PAIRS),
-            array(2 * PAIRS),
-            array(2),
             array(4),
             pltpu.VMEM(flat, jnp.float32),
             pltpu.VMEM(flat, jnp.float32),
             pltpu.VMEM(flat, jnp.float32),
-            array(blocks, WIDE),
+            array(3, WIDE),
             array(NARROW),
-            array(NARROW),
-            array(near, NARROW),
-            array(near, NARROW),
-            array(2, blocks * P_SIZE),
-            array(2, blocks * 4),
-            array(2, blocks * P_SIZE),
-            array(2, blocks * P_SIZE),
-            array(VECS, P_SIZE),
+            array(2, 3, NARROW),
+            array(2),
+            array(2),
+            pltpu.VMEM(flat, jnp.float32),
+            array(4),
+            pltpu.VMEM(flat, jnp.float32),
+            pltpu.VMEM(flat, jnp.float32),
+            array(ITERS, P_SIZE * PAIRS),
             dma((3,)),
             array(VECS, 2),
             array(VECS, 2),
@@ -665,10 +655,12 @@
             dma((VECS, 2)),
             dma((2,)),
             dma((2,)),
-            dma((2, blocks)),
-            dma((2, blocks)),
-            dma((2, 2, near)),
-            dma((2, 2, near)),
+            dma((2, 3)),
+            dma((2, 3)),
+            dma((2, 2, 3)),
+            dma((2, 2, 3)),
+            dma((2,)),
+            dma((2,)),
             dma((2,)),
             dma((2,)),
         ],

time: 38.3 us -> 27.5 us (0.72)
  Pallas kernels: 37.5 us -> 26.6 us
    pallas_call x1, Pallas kernels: 36.6 us -> 25.7 us  [body(): pl.pallas_call(functools.partial(kernel, nx, ny, total), out_shape=(pltpu...]
where the time goes in v2:
time: 27.5 us; the launch traced here: 27.3 us
  Pallas kernels  26.6 us (97%)
  between operations  0.64 us (2%)
    pallas_call x1, Pallas kernels, body(): pl.pallas_call(functools.partial(kernel, nx, ny, total), out_shape=(pltpu...  25.7 us
    pallas_call x1, Pallas kernels, body(): pl.pallas_call(store, out_shape=(jax.ShapeDtypeStruct(hess.shape, jnp.flo...  0.9 us

profile of v2, /device:TPU:0, one launch (start us, length us, event | category | flops | bytes accessed | tf_op | source)
XLA Modules:
  0.0 27.3 jit_solution(17554978917513014412)
XLA Ops:
  0.6 25.7 %shard_map.86 = (f32[6,5]{1,0:T(8,128)S(1)}, f32[6,256,128]{2,1,0:T(8,128)S(1)}) custom-call(f32[8,8]{1,0:T(8,128)} %line.1, f32[8]{0:T(128)} %deriv.1, f32[256,128]{1,0:T(8,128)} %bitcast.4, f32[256,128]{1,0:T(8,128)} %bitcast.5, f32[256,128]{1,0:T(8,128)} %bitcast.6, f32[4,128]{1,0:T(4,128)} %stf.1, s32[4,4,128]{2,1,0:T(4,128)} %wal.1), custom_call_target="tpu_custom_call" | custom-call | tf_op jit(solution)/shard_map/pallas_call | solution.py:622
  26.4 0.9 %shard_map.87 = (f32[6,5]{1,0:T(8,128)}, f32[6,256,128]{2,1,0:T(8,128)}) custom-call(f32[6,5]{1,0:T(8,128)S(1)} %get-tuple-element.6.hess, f32[6,256,128]{2,1,0:T(8,128)S(1)} %get-tuple-element.7.basis), custom_call_target="tpu_custom_call" | custom-call | tf_op jit(solution)/shard_map/pallas_call | solution.py:674

commit v3 on v2

--- a/solution.py
+++ b/solution.py
@@ -23,9 +23,9 @@
 
 def kernel(
     nx, ny, total,
-    line, deriv, src_any, ini_any, rea_any, stf, wal,
+    line_any, deriv_any, src_any, ini_any, rea_any, stf_any, wal_any,
     hess_out, bas,
-    coef, gcoef, small, src, ini, rea,
+    line, deriv, stf, wal, coef, gcoef, small, src, ini, rea,
     wide, narrow, narrow_in, far_send, far_in,
     page_rea, page_small, page_a, page_b, patch,
     in_sem, hsend, hrecv, ysend, yrecv, rsend, rrecv,
@@ -65,11 +65,16 @@
 
     loads = [
         pltpu.make_async_copy(given, held, in_sem.at[k])
-        for k, (given, held) in enumerate(((ini_any, ini), (src_any, src), (rea_any, rea)))
+        for k, (given, held) in enumerate((
+            (ini_any, ini), (line_any, line), (deriv_any, deriv), (stf_any, stf),
+            (wal_any, wal), (src_any, src), (rea_any, rea),
+        ))
     ]
     for load in loads:
         load.start()
     for_peers(greet)
+    for load in loads[1:5]:
+        load.wait()
 
     sub = lax.broadcasted_iota(jnp.int32, (8, 128), 0)
     lane = lax.broadcasted_iota(jnp.int32, (8, 128), 1)
@@ -142,9 +147,10 @@
         return fw, fe
 
     def halo_copy(slot, way, device):
+        rows = pl.ds(0, 3 if slot == 0 else 2)
         return pltpu.make_async_remote_copy(
-            src_ref=hsend.at[slot, way],
-            dst_ref=hrecv.at[slot, way],
+            src_ref=hsend.at[slot, way, rows],
+            dst_ref=hrecv.at[slot, way, rows],
             send_sem=hs_sem.at[slot, way],
             recv_sem=hr_sem.at[slot, way],
             device_id=device,
@@ -159,24 +165,34 @@
             ce = jnp.where(xpos == p, srl(fe[p], p - 3), ce)
         return cw, ce
 
-    def send_halo(slot, faces, ready=lambda: None):
-        cw, ce = pack_faces(faces)
-        hsend[slot, 0] = cw
-        hsend[slot, 1] = ce
+    def halo_copies(slot):
+        return [halo_copy(slot, 0, at(-1, 0)), halo_copy(slot, 1, at(1, 0))]
+
+    def send_halo(slot, faces, ahead, ready=lambda: None):
+        for k, pair in enumerate((pack_faces(faces), pack_faces(ahead))):
+            for way in range(2):
+                hsend[slot, way, k] = pair[way]
+        if slot == 0:
+            hsend[0, 0, 2] = jnp.broadcast_to(small[1, 0:1], (8, 128))
+            hsend[0, 1, 2] = jnp.broadcast_to(small[2, 3:4], (8, 128))
         ready()
-        copies = [halo_copy(slot, 0, at(-1, 0)), halo_copy(slot, 1, at(1, 0))]
-        for copy in copies:
+        for copy in halo_copies(slot):
             copy.start()
-        return copies
-
-    def take_halo(slot, copies, sign):
-        for copy in copies:
-            copy.wait_recv()
-        cw, ce = hrecv[slot, 0], hrecv[slot, 1]
+
+    def inject(cw, ce, sign):
         open_w, open_e = small[1] * sign, small[2] * sign
         first = [open_w * jnp.where(xpos == 0, srl(ce, -p), 0.0) for p in range(PAIRS)]
         last = [open_e * jnp.where(xpos == 3, srl(cw, 3 - p), 0.0) for p in range(PAIRS)]
         return first, last
+
+    def take_halo(slot, sign):
+        for copy in halo_copies(slot):
+            copy.wait_recv()
+        cw, ce = hrecv[slot, 0, 0], hrecv[slot, 1, 0]
+        own_w, own_e = hsend[slot, 0, 0], hsend[slot, 1, 0]
+        ahead_w = hrecv[slot, 0, 1] + (glow[0] * sign) * (hrecv[0, 0, 2] * own_e)
+        ahead_e = hrecv[slot, 1, 1] + (gupp[P_SIZE - 1] * sign) * (hrecv[0, 1, 2] * own_w)
+        return inject(cw, ce, sign), inject(ahead_w, ahead_e, -1.0)
 
     edge_lane = lane == jnp.where(low, 0, 127)
 
@@ -452,60 +468,61 @@
             return v
         return jnp.where(edge, patch[level - 1, a * PAIRS + p], v)
 
-    started = []
+    def finish_rows(ref, first, last):
+        for p in range(PAIRS):
+            put(ref, 0, p, tile(ref, 0, p) + first[p])
+            put(ref, P_SIZE - 1, p, tile(ref, P_SIZE - 1, p) + last[p])
 
     loads[0].wait()
     get = functools.partial(tile, ini)
     faces = xfaces(get)
-    copies = send_halo(0, faces, lambda: pl.semaphore_wait(barrier, n - 1))
-    started += copies
     given = yfaces(get)
-    send_yfaces(given[1])
-    loads[1].wait()
-    loads[2].wait()
+    loads[5].wait()
+    loads[6].wait()
     operate(get, faces, given, lambda a, p, v: put(bas.at[0], a, p, tile(src, a, p) - v))
-    pack_field(rea, P_SIZE, PAIRS)
-    pack_small()
-    for copy in strip_copies(False):
-        copy.start()
 
     late = gy == ny - 1
-    for level in range(ITERS):
-        now = bas.at[level]
-        get = functools.partial(tile, now)
-        fw, fe = xfaces(get)
-        first, last = take_halo(level, copies, 1.0 if level == 0 else -1.0)
-        fw = [fw[p] + glow[0] * first[p] + glow[P_SIZE - 1] * last[p] for p in range(PAIRS)]
-        fe = [fe[p] + gupp[0] * first[p] + gupp[P_SIZE - 1] * last[p] for p in range(PAIRS)]
-        copies = send_halo(level + 1, (fw, fe))
-        started += copies
-        for p in range(PAIRS):
-            put(now, 0, p, get(0, p) + first[p])
-            put(now, P_SIZE - 1, p, get(P_SIZE - 1, p) + last[p])
-        operate(get, (fw, fe), None, functools.partial(put, bas.at[level + 1]))
-        if level == 0:
+    for step in range(VECS // 2):
+        now, after = bas.at[2 * step], bas.at[2 * step + 1]
+        fw, fe = xfaces(functools.partial(tile, now))
+        if step == 0:
+            send_halo(0, faces, (fw, fe), lambda: pl.semaphore_wait(barrier, n - 1))
+            send_yfaces(given[1])
+            pack_field(rea, P_SIZE, PAIRS)
+            pack_small()
+            for copy in strip_copies(False):
+                copy.start()
+        else:
+            send_halo(step, faces, (fw, fe))
+        if step == 1:
             pl.when(jnp.logical_not(late))(finish_first)
-        if level == 1:
-            pl.when(late)(finish_first)
             accs = [None] * 3
             for a, p in tiles():
                 u, v = tile(bas.at[0], a, p), tile(bas.at[1], a, p)
                 new = [u * u, u * v, v * v]
                 accs = new if accs[0] is None else [s + t for s, t in zip(accs, new)]
             start_reduce(0, pack_sums(accs, 0))
-        if level == 2:
+        if step == 2:
+            pl.when(late)(finish_first)
             for copy in strip_copies(False):
                 copy.wait_recv()
             unpack_early()
-        if level == 3:
-            for copy in strip_copies(True):
-                copy.wait_recv()
-            unpack_late()
-            for k in (1, 2, 3):
-                page_level(k)
-        if level == 4:
-            for k in (4, 5):
-                page_level(k)
+        (first, last), extra = take_halo(step, 1.0 if step == 0 else -1.0)
+        fw = [fw[p] + glow[0] * first[p] + glow[P_SIZE - 1] * last[p] for p in range(PAIRS)]
+        fe = [fe[p] + gupp[0] * first[p] + gupp[P_SIZE - 1] * last[p] for p in range(PAIRS)]
+        finish_rows(now, first, last)
+        operate(functools.partial(tile, now), (fw, fe), None, functools.partial(put, after))
+        finish_rows(after, *extra)
+        if step < VECS // 2 - 1:
+            get = functools.partial(tile, after)
+            faces = xfaces(get)
+            operate(get, faces, None, functools.partial(put, bas.at[2 * step + 2]))
+
+    for copy in strip_copies(True):
+        copy.wait_recv()
+    unpack_late()
+    for k in range(1, VECS):
+        page_level(k)
 
     sums = end_reduce(0)
     size = jnp.maximum(sums(0), 1e-30)
@@ -518,8 +535,8 @@
     for k in range(2, VECS):
         powers.append(powers[k - 1] * inv)
 
-    pairs = [(i, j) for j in range(ITERS) for i in range(j + 1)]
-    accs, tail = None, None
+    pairs = [(i, j) for j in range(VECS) for i in range(j + 1)]
+    accs = None
     for a, p in tiles():
         lev = []
         for k in range(VECS):
@@ -531,30 +548,15 @@
             vecs.append(lev[0])
         for k in range(1, VECS):
             put(bas.at[k], a, p, vecs[k])
-        put(bas.at[0], a, p, vecs[0])
         new = [vecs[i] * vecs[j] for i, j in pairs]
         accs = new if accs is None else [s + t for s, t in zip(accs, new)]
-        if 0 < a < P_SIZE - 1:
-            new = [v * vecs[ITERS] for v in vecs]
-            tail = new if tail is None else [s + t for s, t in zip(tail, new)]
-    packed = pack_sums(accs[:8], 0) + pack_sums(accs[8:], 8)
-
-    first, last = take_halo(ITERS, copies, -1.0)
-    for a, extra in ((0, first), (P_SIZE - 1, last)):
-        for p in range(PAIRS):
-            v = tile(bas.at[ITERS], a, p) + jnp.where(edge, 0.0, extra[p] * powers[ITERS])
-            put(bas.at[ITERS], a, p, v)
-            vecs = [tile(bas.at[k], a, p) for k in range(ITERS)] + [v]
-            tail = [s + u * v for s, u in zip(tail, vecs)]
-    start_reduce(1, packed + pack_sums(tail, 16))
+    packed = pack_sums(accs[:8], 0) + pack_sums(accs[8:16], 8) + pack_sums(accs[16:], 16)
+    start_reduce(1, packed)
     sums = end_reduce(1)
 
     gram = {}
     for k, (i, j) in enumerate(pairs):
         gram[i, j] = sums(k) * (1.0 / total)
-    for i in range(VECS):
-        gram[i, ITERS] = sums(16 + i) * (1.0 / total)
-
     def times_gram(u, rows):
         return [
             dot((gram[min(i, r), max(i, r)], u[i]) for i in range(len(u))) for r in range(rows)
@@ -587,7 +589,8 @@
             put(bas.at[j], a, p, dot(zip(combos[j], vecs)))
     hess_out[...] = hess[0:VECS, 0:ITERS]
 
-    for copy in started + y_copies() + strip_copies(False) + strip_copies(True):
+    halos = [copy for slot in range(VECS // 2) for copy in halo_copies(slot)]
+    for copy in halos + y_copies() + strip_copies(False) + strip_copies(True):
         copy.wait_send()
     for slot in range(2):
         block = rrecv.at[slot, pl.ds(0, n - 1)]
@@ -613,7 +616,6 @@
     total = float(nodes * ex * nx * ey * ny)
     vmem = pl.BlockSpec(memory_space=pltpu.VMEM)
     hbm = pl.BlockSpec(memory_space=pl.ANY)
-    smem = pl.BlockSpec(memory_space=pltpu.SMEM)
 
     def array(*lead):
         return pltpu.VMEM(lead + (8, 128), jnp.float32)
@@ -625,9 +627,13 @@
             pltpu.VMEM((VECS, ITERS), jnp.float32),
             pltpu.VMEM((VECS,) + flat, jnp.float32),
         ),
-        in_specs=[smem, smem, hbm, hbm, hbm, vmem, vmem],
+        in_specs=[hbm] * 7,
         out_specs=(vmem, vmem),
         scratch_shapes=[
+            pltpu.SMEM(line_op.shape, jnp.float32),
+            pltpu.SMEM(face_deriv.shape, jnp.float32),
+            pltpu.VMEM(stiffness.shape, jnp.float32),
+            pltpu.VMEM(wall_flags.shape, wall_flags.dtype),
             array(2 * PAIRS * PAIRS),
             array(2 * PAIRS),
             array(4),
@@ -644,15 +650,15 @@
             pltpu.VMEM(flat, jnp.float32),
             pltpu.VMEM(flat, jnp.float32),
             array(ITERS, P_SIZE * PAIRS),
-            dma((3,)),
-            array(VECS, 2),
-            array(VECS, 2),
+            dma((7,)),
+            array(VECS // 2, 2, 3),
+            array(VECS // 2, 2, 3),
             array(),
             array(2),
             pltpu.VMEM((2, 1, 128), jnp.float32),
             pltpu.VMEM((2, n, 128), jnp.float32),
-            dma((VECS, 2)),
-            dma((VECS, 2)),
+            dma((VECS // 2, 2)),
+            dma((VECS // 2, 2)),
             dma((2,)),
             dma((2,)),
             dma((2, 3)),

time: 27.5 us -> 23.9 us (0.87)
  Pallas kernels: 26.6 us -> 23.1 us
    pallas_call x1, Pallas kernels: 25.7 us -> 22.2 us  [body(): pl.pallas_call(functools.partial(kernel, nx, ny, total), out_shape=(pltpu...]
where the time goes in v3:
time: 23.9 us; the launch traced here: 23.8 us
  Pallas kernels  23.1 us (97%)
  between operations  0.64 us (3%)
    pallas_call x1, Pallas kernels, body(): pl.pallas_call(functools.partial(kernel, nx, ny, total), out_shape=(pltpu...  22.2 us
    pallas_call x1, Pallas kernels, body(): pl.pallas_call(store, out_shape=(jax.ShapeDtypeStruct(hess.shape, jnp.flo...  0.9 us

profile of v3, /device:TPU:0, one launch (start us, length us, event | category | flops | bytes accessed | tf_op | source)
XLA Modules:
  0.0 23.8 jit_solution(16843277664827703934)
XLA Ops:
  0.6 22.2 %shard_map.86 = (f32[6,5]{1,0:T(8,128)S(1)}, f32[6,256,128]{2,1,0:T(8,128)S(1)}) custom-call(f32[8,8]{1,0:T(8,128)} %line_any.1, f32[8]{0:T(128)} %deriv_any.1, f32[256,128]{1,0:T(8,128)} %bitcast.4, f32[256,128]{1,0:T(8,128)} %bitcast.5, f32[256,128]{1,0:T(8,128)} %bitcast.6, f32[4,128]{1,0:T(4,128)} %stf_any.1, s32[4,4,128]{2,1,0:T(4,128)} %wal_any.1), custom_call_target="tpu_custom_call" | custom-call | tf_op jit(solution)/shard_map/pallas_call | solution.py:624
  22.9 0.9 %shard_map.87 = (f32[6,5]{1,0:T(8,128)}, f32[6,256,128]{2,1,0:T(8,128)}) custom-call(f32[6,5]{1,0:T(8,128)S(1)} %get-tuple-element.6.hess, f32[6,256,128]{2,1,0:T(8,128)S(1)} %get-tuple-element.7.basis), custom_call_target="tpu_custom_call" | custom-call | tf_op jit(solution)/shard_map/pallas_call | solution.py:680

commit v4 on v3

--- a/solution.py
+++ b/solution.py
@@ -208,18 +208,19 @@
             across.append(halves(lrl(q, 1), lrl(q, 127)))
         return own, across
 
-    def y_copy(target, device):
+    near = (-1, 0, 1)
+    around = [(o, dy) for dy in (-1, 1, 0) for o in near if (o, dy) != (0, 0)]
+
+    def y_copy(o, dy):
+        spot = (1 - dy, near.index(-o))
         return pltpu.make_async_remote_copy(
             src_ref=ysend,
-            dst_ref=yrecv.at[target],
-            send_sem=ys_sem.at[target],
-            recv_sem=yr_sem.at[target],
-            device_id=device,
+            dst_ref=yrecv.at[spot],
+            send_sem=ys_sem.at[spot],
+            recv_sem=yr_sem.at[spot],
+            device_id=at(o, dy),
             device_id_type=MESH,
         )
-
-    def y_copies():
-        return [y_copy(0, at(0, 1)), y_copy(1, at(0, -1))]
 
     def send_yfaces(across):
         packed = across[0]
@@ -227,8 +228,9 @@
             mask = lane == jnp.where(low, a, a - 1)
             packed = jnp.where(mask, lrl(across[a], a), packed)
         ysend[...] = packed
-        for copy in y_copies():
-            copy.start()
+        yrecv[1, 1] = packed
+        for o, dy in around:
+            y_copy(o, dy).start()
 
     def apply(get, react, fields, sides, own, across, emit):
         stiff, open_w, open_e, open_y = fields
@@ -315,8 +317,6 @@
         value = fold(value)
         return lambda k: jnp.broadcast_to(value[:, k:k + 1], (8, 128))
 
-    near = (-1, 0, 1)
-
     def narrow_copy(late, o, dy):
         rows = pl.ds(0, PAIRS) if late else pl.ds(PAIRS, PAIRS + 1)
         side, j = (0 if dy > 0 else 1), near.index(-o)
@@ -355,10 +355,10 @@
 
     def strip_copies(late):
         copies = [narrow_copy(late, o, dy) for dy in (-1, 1) for o in near]
-        copies += [wide_copy(late, o) for o in (-1, 1)]
-        if late:
-            copies += [far_copy(0, -2), far_copy(1, 2)]
-        return copies
+        return copies + [wide_copy(late, o) for o in (-1, 1)]
+
+    def far_copies():
+        return [far_copy(0, -2), far_copy(1, 2)]
 
     def pack_wide(items, index):
         parts = []
@@ -390,9 +390,9 @@
         pack_narrow([items], 2 * PAIRS)
 
     def finish_first():
-        for copy in y_copies():
-            copy.wait_recv()
-        cy = halves(yrecv[0], yrecv[1])
+        for dy in (-1, 1):
+            y_copy(0, dy).wait_recv()
+        cy = halves(yrecv[0, 1], yrecv[2, 1])
         first = bas.at[0]
         for a in range(P_SIZE):
             term = small[3] * jnp.where(edge_lane, lrl(cy, -a), 0.0)
@@ -402,8 +402,7 @@
         cw, ce = pack_faces(xfaces(functools.partial(tile, first)))
         far_send[0] = cw
         far_send[1] = ce
-        pack_field(first, 0, 0)
-        for copy in strip_copies(True):
+        for copy in far_copies():
             copy.start()
 
     def unpack(wide_at, narrow_at, i, p):
@@ -426,8 +425,26 @@
             page_small[f] = unpack(2 * P_SIZE, 2 * PAIRS, 0, f)
 
     def unpack_late():
-        for a, p in tiles():
-            put(page_a, a, p, unpack(a, a // 2, a % 2, p))
+        parts, marks = [], None
+        for j in range(3):
+            for start, lows, upps in (
+                (SLOT * (j + 1), yrecv[0, j], yrecv[1, j]),
+                (64 + SLOT * j + OWNED, yrecv[1, j], yrecv[2, j]),
+            ):
+                parts.append((within(start - 1, P_SIZE + 1), lrl(halves(lows, upps), start)))
+                mark = lane == jnp.where(low, start, start - 1)
+                marks = mark if marks is None else marks | mark
+        lines = overlay(parts)
+        open_y = jnp.where(marks, page_small[3], 0.0)
+        for a in range(P_SIZE):
+            term = open_y * lrl(lines, -a)
+            for p in range(PAIRS):
+                value = unpack(a, a // 2, a % 2, p)
+                if p == 0:
+                    value = value + jnp.where(low, term, 0.0)
+                if p == PAIRS - 1:
+                    value = value + jnp.where(low, 0.0, term)
+                put(page_a, a, p, value)
 
     def page_level(level):
         given, out = (page_a, page_b) if level % 2 else (page_b, page_a)
@@ -481,7 +498,6 @@
     loads[6].wait()
     operate(get, faces, given, lambda a, p, v: put(bas.at[0], a, p, tile(src, a, p) - v))
 
-    late = gy == ny - 1
     for step in range(VECS // 2):
         now, after = bas.at[2 * step], bas.at[2 * step + 1]
         fw, fe = xfaces(functools.partial(tile, now))
@@ -495,7 +511,6 @@
         else:
             send_halo(step, faces, (fw, fe))
         if step == 1:
-            pl.when(jnp.logical_not(late))(finish_first)
             accs = [None] * 3
             for a, p in tiles():
                 u, v = tile(bas.at[0], a, p), tile(bas.at[1], a, p)
@@ -503,7 +518,7 @@
                 accs = new if accs[0] is None else [s + t for s, t in zip(accs, new)]
             start_reduce(0, pack_sums(accs, 0))
         if step == 2:
-            pl.when(late)(finish_first)
+            finish_first()
             for copy in strip_copies(False):
                 copy.wait_recv()
             unpack_early()
@@ -511,6 +526,10 @@
         fw = [fw[p] + glow[0] * first[p] + glow[P_SIZE - 1] * last[p] for p in range(PAIRS)]
         fe = [fe[p] + gupp[0] * first[p] + gupp[P_SIZE - 1] * last[p] for p in range(PAIRS)]
         finish_rows(now, first, last)
+        if step == 0:
+            pack_field(now, 0, 0)
+            for copy in strip_copies(True):
+                copy.start()
         operate(functools.partial(tile, now), (fw, fe), None, functools.partial(put, after))
         finish_rows(after, *extra)
         if step < VECS // 2 - 1:
@@ -518,8 +537,11 @@
             faces = xfaces(get)
             operate(get, faces, None, functools.partial(put, bas.at[2 * step + 2]))
 
-    for copy in strip_copies(True):
+    for copy in strip_copies(True) + far_copies():
         copy.wait_recv()
+    for o, dy in around:
+        if o or not dy:
+            y_copy(o, dy).wait_recv()
     unpack_late()
     for k in range(1, VECS):
         page_level(k)
@@ -590,7 +612,8 @@
     hess_out[...] = hess[0:VECS, 0:ITERS]
 
     halos = [copy for slot in range(VECS // 2) for copy in halo_copies(slot)]
-    for copy in halos + y_copies() + strip_copies(False) + strip_copies(True):
+    edges = strip_copies(False) + strip_copies(True) + far_copies()
+    for copy in halos + edges + [y_copy(o, dy) for o, dy in around]:
         copy.wait_send()
     for slot in range(2):
         block = rrecv.at[slot, pl.ds(0, n - 1)]
@@ -654,13 +677,13 @@
             array(VECS // 2, 2, 3),
             array(VECS // 2, 2, 3),
             array(),
-            array(2),
+            array(3, 3),
             pltpu.VMEM((2, 1, 128), jnp.float32),
             pltpu.VMEM((2, n, 128), jnp.float32),
             dma((VECS // 2, 2)),
             dma((VECS // 2, 2)),
-            dma((2,)),
-            dma((2,)),
+            dma((3, 3)),
+            dma((3, 3)),
             dma((2, 3)),
             dma((2, 3)),
             dma((2, 2, 3)),

time: 23.9 us -> 24.2 us (1.013)
  Pallas kernels: 23.1 us -> 23.4 us
    pallas_call x1, Pallas kernels: 22.2 us -> 22.5 us  [body(): pl.pallas_call(functools.partial(kernel, nx, ny, total), out_shape=(pltpu...]
where the time goes in v4:
time: 24.2 us; the launch traced here: 24.1 us
  Pallas kernels  23.4 us (97%)
  between operations  0.64 us (3%)
    pallas_call x1, Pallas kernels, body(): pl.pallas_call(functools.partial(kernel, nx, ny, total), out_shape=(pltpu...  22.5 us
    pallas_call x1, Pallas kernels, body(): pl.pallas_call(store, out_shape=(jax.ShapeDtypeStruct(hess.shape, jnp.flo...  0.9 us

profile of v4, /device:TPU:0, one launch (start us, length us, event | category | flops | bytes accessed | tf_op | source)
XLA Modules:
  0.0 24.1 jit_solution(4395826913671749243)
XLA Ops:
  0.6 22.5 %shard_map.86 = (f32[6,5]{1,0:T(8,128)S(1)}, f32[6,256,128]{2,1,0:T(8,128)S(1)}) custom-call(f32[8,8]{1,0:T(8,128)} %line_any.1, f32[8]{0:T(128)} %deriv_any.1, f32[256,128]{1,0:T(8,128)} %bitcast.4, f32[256,128]{1,0:T(8,128)} %bitcast.5, f32[256,128]{1,0:T(8,128)} %bitcast.6, f32[4,128]{1,0:T(4,128)} %stf_any.1, s32[4,4,128]{2,1,0:T(4,128)} %wal_any.1), custom_call_target="tpu_custom_call" | custom-call | tf_op jit(solution)/shard_map/pallas_call | solution.py:647
  23.2 0.9 %shard_map.87 = (f32[6,5]{1,0:T(8,128)}, f32[6,256,128]{2,1,0:T(8,128)}) custom-call(f32[6,5]{1,0:T(8,128)S(1)} %get-tuple-element.6.hess, f32[6,256,128]{2,1,0:T(8,128)S(1)} %get-tuple-element.7.basis), custom_call_target="tpu_custom_call" | custom-call | tf_op jit(solution)/shard_map/pallas_call | solution.py:703

commit v5 on v3

--- a/solution.py
+++ b/solution.py
@@ -8,16 +8,16 @@
 from jax.sharding import PartitionSpec as P
 
 P_SIZE = 8
+PAIRS = P_SIZE // 2
 ITERS = 5
 VECS = ITERS + 1
 TAU = 2.0
 FLOOR = 0.1
-PAIRS = P_SIZE // 2
 SLOT = 16
 GHOSTS = ITERS
 OWNED = SLOT - GHOSTS
 WIDE = 2 * P_SIZE + 1
-NARROW = P_SIZE + 1
+NARROW = PAIRS + 1
 MESH = pl.DeviceIdType.MESH
 
 
@@ -318,11 +318,11 @@
     near = (-1, 0, 1)
 
     def narrow_copy(late, o, dy):
-        rows = pl.ds(0, PAIRS) if late else pl.ds(PAIRS, PAIRS + 1)
+        rows = pl.ds(0, 2) if late else pl.ds(2, 3)
         side, j = (0 if dy > 0 else 1), near.index(-o)
         sems = (1 if late else 0, side, j)
         return pltpu.make_async_remote_copy(
-            src_ref=narrow.at[rows],
+            src_ref=narrow.at[side, rows],
             dst_ref=narrow_in.at[side, j, rows],
             send_sem=ns_sem.at[sems],
             recv_sem=nr_sem.at[sems],
@@ -368,26 +368,27 @@
             parts.append((within(spot, SLOT), lrl(v, spot - (128 - OWNED))))
         wide[1, index] = overlay(parts)
 
-    def pack_narrow(pairs, index):
-        parts = []
-        for i, items in enumerate(pairs):
+    def pack_narrow(rows, index):
+        upps, lows = [], []
+        for i, items in enumerate(rows):
             for p, v in enumerate(items):
-                spot = SLOT * p + 8 * i
-                parts.append((within(spot, 8), lrl(v, spot - (128 - GHOSTS))))
-                parts.append((within(64 + spot, 8), lrl(v, 64 + spot)))
-        narrow[index] = overlay(parts)
+                spot = 32 * p + 8 * i
+                upps.append((within(spot, 8), lrl(v, spot - (128 - GHOSTS))))
+                lows.append((within(spot, 8), lrl(v, spot)))
+        narrow[0, index] = overlay(upps)
+        narrow[1, index] = overlay(lows)
 
     def pack_field(ref, wide_at, narrow_at):
         rows = [[tile(ref, a, p) for p in range(PAIRS)] for a in range(P_SIZE)]
         for a in range(P_SIZE):
             pack_wide(rows[a], wide_at + a)
-        for q in range(PAIRS):
-            pack_narrow(rows[2 * q:2 * q + 2], narrow_at + q)
+        for q in range(2):
+            pack_narrow(rows[4 * q:4 * q + 4], narrow_at + q)
 
     def pack_small():
         items = [small[f] for f in range(4)]
         pack_wide(items, 2 * P_SIZE)
-        pack_narrow([items], 2 * PAIRS)
+        pack_narrow([items], PAIRS)
 
     def finish_first():
         for copy in y_copies():
@@ -412,22 +413,22 @@
             mask = within(SLOT * (j + 1), OWNED) | within(64 + SLOT * j, OWNED)
             parts.append((mask, lrl(wide[j, wide_at], SLOT * (j + 1) - 32 * p)))
         for j in range(3):
-            spot = SLOT * j + OWNED
-            both = jnp.where(lane < 64, narrow_in[0, j, narrow_at], narrow_in[1, j, narrow_at])
-            mask = within(spot, GHOSTS) | within(64 + spot, GHOSTS)
-            parts.append((mask, lrl(both, spot - SLOT * p - 8 * i)))
+            for side in range(2):
+                spot = 64 * side + SLOT * j + OWNED
+                v = lrl(narrow_in[side, j, narrow_at], spot - 32 * p - 8 * i)
+                parts.append((within(spot, GHOSTS), v))
         return overlay(parts)
 
     def unpack_early():
         for a, p in tiles():
-            value = unpack(P_SIZE + a, PAIRS + a // 2, a % 2, p)
+            value = unpack(P_SIZE + a, 2 + a // 4, a % 4, p)
             put(page_rea, a, p, value - shift)
         for f in range(4):
-            page_small[f] = unpack(2 * P_SIZE, 2 * PAIRS, 0, f)
+            page_small[f] = unpack(2 * P_SIZE, PAIRS, 0, f)
 
     def unpack_late():
         for a, p in tiles():
-            put(page_a, a, p, unpack(a, a // 2, a % 2, p))
+            put(page_a, a, p, unpack(a, a // 4, a % 4, p))
 
     def page_level(level):
         given, out = (page_a, page_b) if level % 2 else (page_b, page_a)
@@ -488,7 +489,7 @@
         if step == 0:
             send_halo(0, faces, (fw, fe), lambda: pl.semaphore_wait(barrier, n - 1))
             send_yfaces(given[1])
-            pack_field(rea, P_SIZE, PAIRS)
+            pack_field(rea, P_SIZE, 2)
             pack_small()
             for copy in strip_copies(False):
                 copy.start()
@@ -641,7 +642,7 @@
             pltpu.VMEM(flat, jnp.float32),
             pltpu.VMEM(flat, jnp.float32),
             array(3, WIDE),
-            array(NARROW),
+            array(2, NARROW),
             array(2, 3, NARROW),
             array(2),
             array(2),

time: 23.9 us -> 23.8 us (level)
  no operation moved by 1% of the time
where the time goes in v5:
time: 23.8 us; the launch traced here: 23.6 us
  Pallas kernels  23 us (97%)
  between operations  0.64 us (3%)
    pallas_call x1, Pallas kernels, body(): pl.pallas_call(functools.partial(kernel, nx, ny, total), out_shape=(pltpu...  22.1 us
    pallas_call x1, Pallas kernels, body(): pl.pallas_call(store, out_shape=(jax.ShapeDtypeStruct(hess.shape, jnp.flo...  0.9 us

profile of v5, /device:TPU:0, one launch (start us, length us, event | category | flops | bytes accessed | tf_op | source)
XLA Modules:
  0.0 23.6 jit_solution(5729686132817844128)
XLA Ops:
  0.6 22.1 %shard_map.86 = (f32[6,5]{1,0:T(8,128)S(1)}, f32[6,256,128]{2,1,0:T(8,128)S(1)}) custom-call(f32[8,8]{1,0:T(8,128)} %line_any.1, f32[8]{0:T(128)} %deriv_any.1, f32[256,128]{1,0:T(8,128)} %bitcast.4, f32[256,128]{1,0:T(8,128)} %bitcast.5, f32[256,128]{1,0:T(8,128)} %bitcast.6, f32[4,128]{1,0:T(4,128)} %stf_any.1, s32[4,4,128]{2,1,0:T(4,128)} %wal_any.1), custom_call_target="tpu_custom_call" | custom-call | tf_op jit(solution)/shard_map/pallas_call | solution.py:625
  22.7 0.9 %shard_map.87 = (f32[6,5]{1,0:T(8,128)}, f32[6,256,128]{2,1,0:T(8,128)}) custom-call(f32[6,5]{1,0:T(8,128)S(1)} %get-tuple-element.6.hess, f32[6,256,128]{2,1,0:T(8,128)S(1)} %get-tuple-element.7.basis), custom_call_target="tpu_custom_call" | custom-call | tf_op jit(solution)/shard_map/pallas_call | solution.py:681

commit v6 on v5

--- a/solution.py
+++ b/solution.py
@@ -324,7 +324,7 @@
         return pltpu.make_async_remote_copy(
             src_ref=narrow.at[side, rows],
             dst_ref=narrow_in.at[side, j, rows],
-            send_sem=ns_sem.at[sems],
+            send_sem=ns_sem.at[0],
             recv_sem=nr_sem.at[sems],
             device_id=at(o, dy),
             device_id_type=MESH,
@@ -337,7 +337,7 @@
         return pltpu.make_async_remote_copy(
             src_ref=wide.at[1, rows],
             dst_ref=wide.at[j, rows],
-            send_sem=ws_sem.at[sems],
+            send_sem=ws_sem.at[0],
             recv_sem=wr_sem.at[sems],
             device_id=at(o, 0),
             device_id_type=MESH,
@@ -591,8 +591,10 @@
     hess_out[...] = hess[0:VECS, 0:ITERS]
 
     halos = [copy for slot in range(VECS // 2) for copy in halo_copies(slot)]
-    for copy in halos + y_copies() + strip_copies(False) + strip_copies(True):
+    for copy in halos + y_copies() + [far_copy(0, -2), far_copy(1, 2)]:
         copy.wait_send()
+    for block, sem in ((narrow_in, ns_sem), (wide.at[pl.ds(0, 2)], ws_sem)):
+        pltpu.make_async_copy(block, block, sem.at[0]).wait()
     for slot in range(2):
         block = rrecv.at[slot, pl.ds(0, n - 1)]
         pltpu.make_async_copy(block, block, rs_sem.at[slot]).wait()
@@ -662,9 +664,9 @@
             dma((VECS // 2, 2)),
             dma((2,)),
             dma((2,)),
+            dma((1,)),
             dma((2, 3)),
-            dma((2, 3)),
-            dma((2, 2, 3)),
+            dma((1,)),
             dma((2, 2, 3)),
             dma((2,)),
             dma((2,)),

time: 23.8 us -> 23.6 us (level)
  no operation moved by 1% of the time
where the time goes in v6:
time: 23.6 us; the launch traced here: 23.5 us
  Pallas kernels  22.8 us (97%)
  between operations  0.64 us (3%)
    pallas_call x1, Pallas kernels, body(): pl.pallas_call(functools.partial(kernel, nx, ny, total), out_shape=(pltpu...  21.9 us
    pallas_call x1, Pallas kernels, body(): pl.pallas_call(store, out_shape=(jax.ShapeDtypeStruct(hess.shape, jnp.flo...  0.9 us

profile of v6, /device:TPU:0, one launch (start us, length us, event | category | flops | bytes accessed | tf_op | source)
XLA Modules:
  0.0 23.5 jit_solution(2237591543027187646)
XLA Ops:
  0.6 21.9 %shard_map.86 = (f32[6,5]{1,0:T(8,128)S(1)}, f32[6,256,128]{2,1,0:T(8,128)S(1)}) custom-call(f32[8,8]{1,0:T(8,128)} %line_any.1, f32[8]{0:T(128)} %deriv_any.1, f32[256,128]{1,0:T(8,128)} %bitcast.4, f32[256,128]{1,0:T(8,128)} %bitcast.5, f32[256,128]{1,0:T(8,128)} %bitcast.6, f32[4,128]{1,0:T(4,128)} %stf_any.1, s32[4,4,128]{2,1,0:T(4,128)} %wal_any.1), custom_call_target="tpu_custom_call" | custom-call | tf_op jit(solution)/shard_map/pallas_call | solution.py:627
  22.6 0.9 %shard_map.87 = (f32[6,5]{1,0:T(8,128)}, f32[6,256,128]{2,1,0:T(8,128)}) custom-call(f32[6,5]{1,0:T(8,128)S(1)} %get-tuple-element.6.hess, f32[6,256,128]{2,1,0:T(8,128)S(1)} %get-tuple-element.7.basis), custom_call_target="tpu_custom_call" | custom-call | tf_op jit(solution)/shard_map/pallas_call | solution.py:683
